TPU v7x, 128 devices: a whole 4x4x4 slice. The times are simulated.
128 devices in a mesh: img: 8 (over y, core), cell: 16 (over z, x).
Axes of the slice: x: 4, y: 4, z: 4, core: 2. Of those that a mesh axis runs over, the one named last changes fastest.
Arguments:
- attributes: float32 [59, 1048576], P(None, ('img', 'cell')), may hold values from -5 to 2, as said below
- camera: float32 [3, 3], replicated, may hold values from -6 to 5, as said below
- target: float32 [3, 256, 4096], P(None, 'img', 'cell'), may hold values from 0 to 1
- visible_index: int32 [128, 8192], P(('img', 'cell')), may hold values from 0 to 8191
- tile_lists: int32 [16, 256, 128], P('img', 'cell'), may hold values from 0 to 8191
- tile_len: int32 [16, 256], P('img', 'cell'), may hold values from 16 to 128
Outputs:
- gradient: float32 [59, 1048576], P(None, ('img', 'cell'))
Inputs may be any that keep to these rules, and one draw needn't show every extreme that they name: `attributes`: rows 0 to 2 (positions) lie within [-1, 1]. `camera`: row 2, the eye, lies 4 or more from the anchor.
All inputs are finite; a program needn't handle non-finite values.
Results may differ from a plain program's by a relative error of at most 0.0003.
Values sent between devices are 32-bit elements; how exact they have to be, the bound alone decides.
A program may use at most 64 MiB of HBM per device.

v0:
```python
import math

import jax
import jax.numpy as jnp
from jax import lax
from jax.sharding import PartitionSpec as P

TILE = 16


WEIGHT_SSIM = 0.2
SMOOTHING = 0.01
STAB_ONE = 0.0001
STAB_TWO = 0.0009
BLUR_SIGMA = 1.5
rim_width = 5
SH_ZERO = 0.28209479177387814
SH_ONE = 0.4886025119029199
SH_TWO = (
    1.0925484305920792,
    -1.0925484305920792,
    0.31539156525252005,
    -1.0925484305920792,
    0.5462742152960396,
)
SH_THREE = (
    -0.5900435899266435,
    2.890611442640554,
    -0.4570457994644658,
    0.3731763325901154,
    -0.4570457994644658,
    1.445305721320277,
    -0.5900435899266435,
)


def extended(block, sides, width):
    for axis, dim in sides:
        count = lax.axis_size(axis)
        forward = [(i, i + 1) for i in range(count - 1)]
        backward = [(target, source) for source, target in forward]
        low = lax.ppermute(
            lax.slice_in_dim(block, block.shape[dim] - width, None, axis=dim), axis, forward
        )
        high = lax.ppermute(lax.slice_in_dim(block, 0, width, axis=dim), axis, backward)
        block = jnp.concatenate([low, block, high], axis=dim)
    return block


def harmonic_basis(unit_x, unit_y, unit_z):
    unit_xx = unit_x * unit_x
    unit_yy = unit_y * unit_y
    unit_zz = unit_z * unit_z
    return [
        SH_ZERO + 0.0 * unit_x,
        -SH_ONE * unit_y,
        SH_ONE * unit_z,
        -SH_ONE * unit_x,
        SH_TWO[0] * unit_x * unit_y,
        SH_TWO[1] * unit_y * unit_z,
        SH_TWO[2] * (2.0 * unit_zz - unit_xx - unit_yy),
        SH_TWO[3] * unit_x * unit_z,
        SH_TWO[4] * (unit_xx - unit_yy),
        SH_THREE[0] * unit_y * (3.0 * unit_xx - unit_yy),
        SH_THREE[1] * unit_x * unit_y * unit_z,
        SH_THREE[2] * unit_y * (4.0 * unit_zz - unit_xx - unit_yy),
        SH_THREE[3] * unit_z * (2.0 * unit_zz - 3.0 * unit_xx - 3.0 * unit_yy),
        SH_THREE[4] * unit_x * (4.0 * unit_zz - unit_xx - unit_yy),
        SH_THREE[5] * unit_z * (unit_xx - unit_yy),
        SH_THREE[6] * unit_x * (unit_xx - 3.0 * unit_yy),
    ]


def project_rows(attr_rows, camera):
    positions = [attr_rows[number] for number in range(3)]
    scales = [jnp.exp(attr_rows[3 + number]) for number in range(3)]
    quat_w = 1.5 + jnp.tanh(attr_rows[6])
    quat_x = attr_rows[7]
    quat_y = attr_rows[8]
    quat_z = attr_rows[9]
    length = jnp.sqrt(quat_w * quat_w + quat_x * quat_x + quat_y * quat_y + quat_z * quat_z)
    quat_w, quat_x, quat_y, quat_z = (
        quat_w / length,
        quat_x / length,
        quat_y / length,
        quat_z / length,
    )
    rotation = [
        [
            1.0 - 2.0 * (quat_y * quat_y + quat_z * quat_z),
            2.0 * (quat_x * quat_y - quat_w * quat_z),
            2.0 * (quat_x * quat_z + quat_w * quat_y),
        ],
        [
            2.0 * (quat_x * quat_y + quat_w * quat_z),
            1.0 - 2.0 * (quat_x * quat_x + quat_z * quat_z),
            2.0 * (quat_y * quat_z - quat_w * quat_x),
        ],
        [
            2.0 * (quat_x * quat_z - quat_w * quat_y),
            2.0 * (quat_y * quat_z + quat_w * quat_x),
            1.0 - 2.0 * (quat_x * quat_x + quat_y * quat_y),
        ],
    ]
    screen_axes = [
        [
            sum(
                (
                    camera[screen_axis, world_axis] * rotation[world_axis][scale_axis]
                    for world_axis in range(3)
                )
            )
            * scales[scale_axis]
            for scale_axis in range(3)
        ]
        for screen_axis in range(2)
    ]
    cov_first = (
        sum((screen_axes[0][scale_axis] * screen_axes[0][scale_axis] for scale_axis in range(3)))
        + 0.3
    )
    cov_mixed = sum(
        (screen_axes[0][scale_axis] * screen_axes[1][scale_axis] for scale_axis in range(3))
    )
    cov_second = (
        sum((screen_axes[1][scale_axis] * screen_axes[1][scale_axis] for scale_axis in range(3)))
        + 0.3
    )
    determinant = cov_first * cov_second - cov_mixed * cov_mixed
    centers = [
        8.0
        + 7.0
        * jnp.sin(
            sum(
                (camera[screen_axis, world_axis] * positions[world_axis] for world_axis in range(3))
            )
            / 3.0
        )
        for screen_axis in range(2)
    ]
    offsets = [positions[world_axis] - camera[2, world_axis] for world_axis in range(3)]
    distance = jnp.sqrt(offsets[0] * offsets[0] + offsets[1] * offsets[1] + offsets[2] * offsets[2])
    basis = harmonic_basis(offsets[0] / distance, offsets[1] / distance, offsets[2] / distance)
    harmonics = attr_rows[11:].reshape((3, 16) + attr_rows.shape[1:])
    colours = [
        0.5 + sum((basis[term] * harmonics[channel, term] for term in range(16)))
        for channel in range(3)
    ]
    opacity = jax.nn.sigmoid(attr_rows[10])
    return jnp.stack(
        centers
        + [cov_second / determinant, -cov_mixed / determinant, cov_first / determinant, opacity]
        + colours
    )


def render_block(tile_feats, live_mask):
    pixels = jnp.arange(TILE * TILE, dtype=jnp.int32)
    pixel_x = (pixels % TILE).astype(jnp.float32) + 0.5
    pixel_y = (pixels // TILE).astype(jnp.float32) + 0.5
    delta_x = pixel_x[None, None, :] - tile_feats[0][:, :, None]
    delta_y = pixel_y[None, None, :] - tile_feats[1][:, :, None]
    exponent = -0.5 * (
        tile_feats[2][:, :, None] * delta_x * delta_x
        + 2.0 * tile_feats[3][:, :, None] * delta_x * delta_y
        + tile_feats[4][:, :, None] * delta_y * delta_y
    )
    opacity_map = (live_mask * tile_feats[5])[:, :, None] * jnp.exp(exponent)
    log_keep = jnp.log1p(-opacity_map)
    before = jnp.cumsum(log_keep, axis=1) - log_keep
    weight = jnp.exp(before) * opacity_map
    return jnp.einsum("cbk,bkp->cbp", tile_feats[6:9], weight, precision=lax.Precision.HIGHEST)


def render_pair(block_pair):
    return render_block(block_pair[0], block_pair[1])


def render_back(triple):
    feats_in, mask_in, cotangent = triple

    def render_with(feats_now):
        return render_block(feats_now, mask_in)

    rendered, pullback = jax.vjp(render_with, feats_in)
    return pullback(cotangent)[0]


def band_matrix(count):
    rows_at = jnp.arange(count, dtype=jnp.int32)[:, None]
    cols_at = jnp.arange(count + 10, dtype=jnp.int32)[None, :]
    offset = cols_at - rows_at
    inside = (offset >= 0) & (offset <= 10)
    shifted = (offset - 5).astype(jnp.float32)
    tap_offsets = jnp.arange(11, dtype=jnp.float32) - 5.0
    norm_total = jnp.sum(jnp.exp(-tap_offsets * tap_offsets / (2.0 * BLUR_SIGMA * BLUR_SIGMA)))
    values = jnp.exp(-shifted * shifted / (2.0 * BLUR_SIGMA * BLUR_SIGMA)) / norm_total
    return jnp.where(inside, values, 0.0)


def blur_block(padded):
    height = padded.shape[1] - 10
    breadth = padded.shape[2] - 10
    downward = band_matrix(height)
    sideways = band_matrix(breadth)
    partial_rows = jnp.einsum("ij,kjl->kil", downward, padded, precision=lax.Precision.HIGHEST)
    return jnp.einsum("kil,ml->kim", partial_rows, sideways, precision=lax.Precision.HIGHEST)


def ssim_value(mean_render, mean_target, square_render, square_target, cross_term):
    spread_render = square_render - mean_render * mean_render
    spread_target = square_target - mean_target * mean_target
    covariance = cross_term - mean_render * mean_target
    upper = (2.0 * mean_render * mean_target + STAB_ONE) * (2.0 * covariance + STAB_TWO)
    lower = (mean_render * mean_render + mean_target * mean_target + STAB_ONE) * (
        spread_render + spread_target + STAB_TWO
    )
    return upper / lower


def route_requests(payload):
    return lax.all_to_all(payload, ("img", "cell"), split_axis=1, concat_axis=1, tiled=True)


def route_replies(payload):
    return lax.all_to_all(payload, ("img", "cell"), split_axis=1, concat_axis=1, tiled=True)


def route_returns(payload):
    return lax.all_to_all(payload, ("img", "cell"), split_axis=1, concat_axis=1, tiled=True)


def shards(attributes, camera, target, visible_index, tile_lists, tile_len):
    img_count = lax.axis_size("img")
    cell_count = lax.axis_size("cell")
    devices = img_count * cell_count
    slots = visible_index.shape[1]
    per_owner = slots // devices
    received = route_requests(visible_index.reshape(1, devices, per_owner))[0]
    owner_rows = jnp.take(attributes, received, axis=1)

    def project_with(attr_rows):
        return project_rows(attr_rows, camera)

    outgoing_data, owner_pullback = jax.vjp(project_with, owner_rows)
    arrived = route_replies(outgoing_data)
    feat_count = arrived.shape[0]
    feature_flat = arrived.reshape(feat_count, slots)
    tiles_down = tile_lists.shape[0]
    tiles_across = tile_lists.shape[1]
    list_length = tile_lists.shape[2]
    tile_count = tiles_down * tiles_across
    entry_ids = tile_lists.reshape(tile_count, list_length)
    live_mask = (
        jnp.arange(list_length, dtype=jnp.int32)[None, :] < tile_len.reshape(tile_count, 1)
    ).astype(jnp.float32)
    block_size = math.gcd(tile_count, 32)
    block_total = tile_count // block_size
    tile_feats = (
        jnp.take(feature_flat, entry_ids, axis=1)
        .reshape(feat_count, block_total, block_size, list_length)
        .transpose(1, 0, 2, 3)
    )
    masks = live_mask.reshape(block_total, block_size, list_length)
    rendered = lax.map(render_pair, (tile_feats, masks))
    render_image = (
        rendered.transpose(1, 0, 2, 3)
        .reshape(3, tiles_down, tiles_across, TILE, TILE)
        .transpose(0, 1, 3, 2, 4)
    )
    render_image = render_image.reshape(3, tiles_down * TILE, tiles_across * TILE)
    both_pads = extended(jnp.stack([render_image, target]), (("img", 2), ("cell", 3)), rim_width)
    render_pad = both_pads[0]
    target_pad = both_pads[1]
    filtered = blur_block(
        jnp.concatenate(
            [
                render_pad,
                target_pad,
                render_pad * render_pad,
                target_pad * target_pad,
                render_pad * target_pad,
            ]
        )
    )
    mean_render, mean_target, square_render, square_target, cross_term = jnp.split(filtered, 5)

    def similarity_of(mean_value, square_value, cross_value):
        return ssim_value(mean_value, mean_target, square_value, square_target, cross_value)

    similarity, ssim_pullback = jax.vjp(similarity_of, mean_render, square_render, cross_term)
    coef_mean, coef_square, coef_cross = ssim_pullback(jnp.full_like(similarity, -WEIGHT_SSIM))
    coef_pads = extended(
        jnp.concatenate([coef_mean, coef_square, coef_cross]), (("img", 1), ("cell", 2)), rim_width
    )
    back_mean, back_square, back_cross = jnp.split(blur_block(coef_pads), 3)
    difference = render_image - target
    image_grad = (
        (1.0 - WEIGHT_SSIM) * difference / jnp.sqrt(difference * difference + SMOOTHING * SMOOTHING)
        + back_mean
        + 2.0 * render_image * back_square
        + target * back_cross
    )
    grad_tiles = image_grad.reshape(3, tiles_down, TILE, tiles_across, TILE).transpose(
        0, 1, 3, 2, 4
    )
    grad_tiles = grad_tiles.reshape(3, block_total, block_size, TILE * TILE).transpose(1, 0, 2, 3)
    feature_grads = lax.map(render_back, (tile_feats, masks, grad_tiles))
    feature_grads = feature_grads.transpose(1, 0, 2, 3).reshape(feat_count, tile_count, list_length)
    slot_grads = jnp.zeros((feat_count, slots), jnp.float32).at[:, entry_ids].add(feature_grads)
    slot_grads = slot_grads.reshape(feat_count, devices, per_owner)
    returned = route_returns(slot_grads)
    row_grads = owner_pullback(returned)[0]
    gradient = (
        jnp.zeros_like(attributes)
        .at[:, received.reshape(-1)]
        .add(row_grads.reshape(row_grads.shape[0], devices * per_owner))
    )
    return gradient


def solution(mesh):
    return jax.shard_map(
        shards,
        mesh=mesh,
        in_specs=(
            P(None, ("img", "cell")),
            P(),
            P(None, "img", "cell"),
            P(("img", "cell"), None),
            P("img", "cell", None),
            P("img", "cell"),
        ),
        out_specs=P(None, ("img", "cell")),
        check_vma=False,
    )
```

profile of v0, /device:TPU:1, one launch (start us, length us, event | category | flops | bytes accessed | tf_op | source)
XLA Modules:
  0.0 429.7 jit_solution(15723929564303703378)
XLA Ops:
  2.7 11.5 %all-to-all-start = ((s32[1,128,64]{2,0,1:T(1,128)}), s32[1,128,64]{2,0,1:T(1,128)S(1)}, u32[]{:S(2)}, u32[]{:S(2)}) async-start(s32[1,128,64]{2,0,1:T(1,128)} %bitcast), calls=%async_computation | async-start | bytes 131072 | tf_op jit(solution)/shard_map/all_to_all | solution.py:222
  22.3 3.9 copy.175
  26.5 30.1 %gather_fusion = f32[8192,59]{1,0:T(8,128)} fusion(f32[59,8192]{0,1:T(8,128)} %copy.175, s32[8192]{0:T(1024)S(1)} %broadcast_clamp_fusion), kind=kCustom, calls=%fused_computation | custom fusion | bytes 3899392 | tf_op jit(solution)/shard_map/jit(_take)/gather | solution.py:240
  56.6 5.3 %copy.176 = f32[128,64,59]{0,1,2:T(8,128)} copy(f32[128,64,59]{2,1,0:T(8,128)} %bitcast.577) | data formatting | bytes 3866624 | tf_op jit(solution)/shard_map/jit(_take)/gather | solution.py:240
  61.8 1.7 select_bitcast_fusion
  63.5 2.8 fusion.204
  66.5 2.6 fusion.206
  69.1 4.7 %divide_dynamic-update-slice_fusion.2 = (f32[9,128,64]{1,2,0:T(8,128)}, f32[1,128,64]{1,2,0:T(8,128)S(1)}, f32[1,128,64]{1,2,0:T(8,128)S(1)}, f32[1,128,64]{1,2,...) fusion(f32[9,128,64]{1,2,0:T(8,128)} %get-tuple-element.136, ...), kind=kLoop, calls=%fused_computation.375 | loop fusion | flops 614400 | bytes 953368
  75.6 2.6 add_dynamic-update-slice_fusion.2
  79.7 2.3 copy.177
  82.0 2.4 reshape.1816
  84.4 10.8 %all-to-all-start.1 = ((f32[128,1,576]{2,1,0:T(1,128)}), f32[128,1,576]{2,1,0:T(1,128)}, u32[]{:S(2)}, u32[]{:S(2)}) async-start(f32[128,1,576]{2,1,0:T(1,128)} %reshape.1816), calls=%async_computation.1 | async-start | bytes 655360 | tf_op jit(solution)/shard_map/all_to_all | solution.py:226
  96.4 10.4 %all-to-all-done.1 = f32[128,1,576]{2,1,0:T(1,128)} async-done(((f32[128,1,576]{2,1,0:T(1,128)}), f32[128,1,576]{2,1,0:T(1,128)}, u32[]{:S(2)}, u32[]{:S(2)}) %all-to-all-start.1) | async-done | bytes 294944 | tf_op jit(solution)/shard_map/all_to_all | solution.py:226
  107.4 3.1 reduce.8
  110.5 2.1 reshape.1817
  112.6 3.8 copy.178
  116.4 16.4 %gather_fusion.1 = f32[4096,9]{1,0:T(8,128)} fusion(f32[9,8192]{0,1:T(8,128)} %bitcast.583, s32[4096]{0:T(1024)S(1)} %copy-done.61), kind=kCustom, calls=%fused_computation.1 | custom fusion | bytes 311296 | tf_op jit(solution)/shard_map/jit(_take)/gather | solution.py:260
  132.8 2.9 copy.180
  137.5 4.1 negate_log-plus-one_fusion
  141.7 2.5 fusion.22
  144.3 8.7 %fusion.30 = f32[3,32,256]{2,0,1:T(4,128)S(1)} fusion(f32[32,128]{1,0:T(8,128)S(1)} %bitcast.599, f32[32,128]{1,0:T(8,128)S(1)} %bitcast.604, f32[256]{0:T(256)S(1)} %copy-done.62, f32[32,128]{1,0:T(8,128)S(1)} %bitcast.609, f32[32,128]{1,0:T(8,128)S(1)} %bitcast.614, f32[256]{0:T(256)S(1)} %copy-done.64, f32[32,128]{1,0:T(8,128)S(1)} %bitcast.619, ...), kind=kOutput, calls=%fused_computation.57 | convolution fusion | flops 53477376 | bytes 4458496 | tf_op jit(solution)/shard_map/while/body/eval_jaxpr/cbk,bkp->cbp/dot_general | solution.py:172
  153.7 2.0 reshape_transpose.4
  155.7 2.3 copy.184
  158.0 2.1 stack_reshape.3
  160.9 2.6 collective-permute-start
  163.6 1.9 collective-permute-start.1
  165.5 3.5 collective-permute-done.1
  170.0 2.3 collective-permute-start.2
  174.4 3.9 collective-permute-done.3
  183.1 3.7 collective-permute-start.4
  186.7 1.9 collective-permute-start.5
  188.7 3.7 collective-permute-done.5
  193.3 2.9 collective-permute-start.6
  201.9 2.3 reduce.7
  205.7 2.1 reshape.1754
  207.8 2.8 convolution_bitcast_fusion.1
  213.6 2.0 reshape.1755
  215.7 2.3 copy.250
  218.0 2.1 squeeze.314
  220.1 10.1 %fusion.31 = f32[3,32,128]{2,0,1:T(4,128)S(1)} fusion(f32[32,128]{1,0:T(8,128)S(1)} %bitcast.600, f32[32,128]{1,0:T(8,128)} %bitcast.605, f32[256]{0:T(256)} %get-tuple-element.236, f32[32,128]{1,0:T(8,128)} %bitcast.610, f32[32,128]{1,0:T(8,128)} %bitcast.615, f32[256]{0:T(256)} %get-tuple-element.237, f32[32,128]{1,0:T(8,128)} %bitcast.620, ...), kind=kOutput, calls=%fused_computation.58 | convolution fusion | flops 53477376 | bytes 4442112 | tf_op jit(solution)/shard_map/while/body/eval_jaxpr/transpose(jvp(cbk,bkp->cbp))/dot_general | solution.py:172
  230.3 9.0 %multiply_multiply_fusion.1 = (f32[32,128,256]{2,1,0:T(8,128)S(1)}, f32[32,128,256]{2,1,0:T(8,128)S(1)}) fusion(f32[32,128]{1,0:T(8,128)S(1)} %bitcast.601, f32[32,128]{1,0:T(8,128)S(1)} %bitcast.606, f32[256]{0:T(256)S(1)} %copy-done.63, f32[32,128]{1,0:T(8,128)S(1)} %bitcast.611, f32[32,128]{1,0:T(8,128)S(1)} %bitcast.616, f32[256]{0:T(256)S(1)} %copy-done.65, ...), kind=kOutput, calls=%fused_computation.43 | convolution fusion | flops 54525952 | bytes 12847104 | tf_op jit(solution)/shard_map/while/body/eval_jaxpr/transpose(jvp(cbk,bkp->cbp))/dot_general | solution.py:172
  239.3 10.3 %fusion.19 = f32[32,128,256]{2,0,1:T(8,128)S(1)} fusion(f32[32,128,256]{2,1,0:T(8,128)S(1)} %get-tuple-element.234), kind=kOutput, calls=%fused_computation.35 | output fusion | flops 133169152 | bytes 8388608 | tf_op jit(solution)/shard_map/while/body/eval_jaxpr/transpose(jvp(jit(cumsum)))/reduce_window_sum | solution.py:170
  249.7 16.0 %fusion.13 = (f32[32,128]{1,0:T(8,128)S(1)}, f32[32,128]{1,0:T(8,128)S(1)}, f32[32,128]{1,0:T(8,128)S(1)}, f32[32,128]{1,0:T(8,128)S(1)}, f32[32,128]{1,0:T(8,128)S(1)}, /*index=5*/f32[32,128]{1,0:T(8,128)S(1)}) fusion(f32[32,128]{1,0:T(8,128)S(1)} %bitcast.607, f32[256]{0:T(256)S(1)} %copy-done.63, f32[32,128]{1,0:T(8,128)S(1)} %bitcast.602, ...), kind=kLoop, calls=%fused_computation.28 | loop fusion | flops 50307072 | bytes 12781568 | tf_op jit(solution)/shard_map/while/body/eval_jaxpr/transpose(jvp())/reduce_sum | solution.py:166
  266.7 2.9 copy.208
  269.6 24.9 %scatter_custom_fusion = f32[9,8192]{0,1:T(8,128)} fusion(s32[4096]{0:T(1024)} %fusion.129, f32[4096,9]{1,0:T(8,128)} %bitcast.592, f32[]{:T(128)} %constant.104.clone.1), kind=kCustom, calls=%fused_computation.46 | custom fusion | flops 36864 | bytes 295424 | tf_op jit(solution)/shard_map/scatter-add | solution.py:310
  294.5 3.8 copy.193
  298.3 2.4 reshape.1818
  300.7 10.4 %all-to-all-start.2 = ((f32[128,1,576]{2,1,0:T(1,128)}), f32[128,1,576]{2,1,0:T(1,128)}, u32[]{:S(2)}, u32[]{:S(2)}) async-start(f32[128,1,576]{2,1,0:T(1,128)} %reshape.1818), calls=%async_computation.2 | async-start | bytes 655360 | tf_op jit(solution)/shard_map/all_to_all | solution.py:230
  312.5 10.2 %all-to-all-done.2 = f32[128,1,576]{2,1,0:T(1,128)} async-done(((f32[128,1,576]{2,1,0:T(1,128)}), f32[128,1,576]{2,1,0:T(1,128)}, u32[]{:S(2)}, u32[]{:S(2)}) %all-to-all-start.2) | async-done | bytes 294944 | tf_op jit(solution)/shard_map/all_to_all | solution.py:230
  322.7 3.1 reduce.9
  325.8 2.1 reshape.1819
  327.9 4.3 %fusion.207 = (f32[1,128,64]{2,0,1:T(1,128)}, f32[1,128,64]{2,0,1:T(1,128)}, f32[1,128,64]{2,0,1:T(1,128)}, f32[1,128,64]{2,0,1:T(1,128)}, f32[1,128,64]{2,0,1:T...) fusion(f32[9,128,64]{2,0,1:T(8,128)} %bitcast.590), kind=kLoop, calls=%fused_computation.498 | loop fusion | bytes 589824 | tf_op jit(solution)/shard_map/transpose(jvp())/unstack | solution.py:150
  346.2 2.8 bitcast_multiply_fusion.47
  349.1 3.3 fusion.92
  352.3 3.0 fusion.94
  355.4 3.0 fusion.96
  358.4 1.9 bitcast_multiply_fusion.46
  360.5 3.9 add_add_fusion.14
  364.4 3.9 add_add_fusion.11
  369.5 3.1 copy.203
  372.6 3.4 reshape.1784
  376.0 2.8 copy.204
  378.9 46.5 %scatter_custom_fusion.1 = f32[59,8192]{0,1:T(8,128)} fusion(s32[8192]{0:T(1024)} %bitcast.632, f32[8192,59]{1,0:T(8,128)} %copy.204, f32[]{:T(128)} %constant.104.clone.1), kind=kCustom, calls=%fused_computation.48 | custom fusion | flops 483328 | bytes 1933824 | tf_op jit(solution)/shard_map/scatter-add | solution.py:317
  425.4 3.8 copy.205
  (209 shorter events, 48.3 us)
Async XLA Ops:
  2.7 23.5 %all-to-all-start = ((s32[1,128,64]{2,0,1:T(1,128)}), s32[1,128,64]{2,0,1:T(1,128)S(1)}, u32[]{:S(2)}, u32[]{:S(2)}) async-start(s32[1,128,64]{2,0,1:T(1,128)} %bitcast), calls=%async_computation | async-start | bytes 131072 | tf_op jit(solution)/shard_map/all_to_all | solution.py:222
  26.2 30.3 %copy-start.4 = (s32[1,128,64]{2,0,1:T(1,128)}, s32[1,128,64]{2,0,1:T(1,128)S(1)}, u32[]{:S(2)}) copy-start(s32[1,128,64]{2,0,1:T(1,128)S(1)} %all-to-all-done) | copy-start | bytes 98308
  66.3 9.3 %copy-start.9 = (f32[1,128,64]{1,2,0:T(8,128)}, f32[1,128,64]{1,2,0:T(8,128)S(1)}, u32[]{:S(2)}) copy-start(f32[1,128,64]{1,2,0:T(8,128)S(1)} %get-tuple-element.114) | copy-start | bytes 98308
  66.3 12.0 %copy-start.17 = (f32[1,128,64]{1,2,0:T(8,128)}, f32[1,128,64]{1,2,0:T(8,128)S(1)}, u32[]{:S(2)}) copy-start(f32[1,128,64]{1,2,0:T(8,128)S(1)} %get-tuple-element.115) | copy-start | bytes 98308
  66.3 12.0 %copy-start.19 = (f32[1,128,64]{1,2,0:T(8,128)}, f32[1,128,64]{1,2,0:T(8,128)S(1)}, u32[]{:S(2)}) copy-start(f32[1,128,64]{1,2,0:T(8,128)S(1)} %get-tuple-element.113) | copy-start | bytes 98308
  66.5 29.3 %copy-start.45 = (s32[2,16,128]{2,1,0:T(8,128)S(1)}, s32[2,16,128]{2,1,0:T(8,128)}, u32[]{:S(2)}) copy-start(s32[2,16,128]{2,1,0:T(8,128)} %param.10) | copy-start | bytes 49156
  69.1 9.2 %copy-start.13 = (f32[1,128,64]{1,2,0:T(8,128)}, f32[1,128,64]{1,2,0:T(8,128)S(1)}, u32[]{:S(2)}) copy-start(f32[1,128,64]{1,2,0:T(8,128)S(1)} %get-tuple-element.118) | copy-start | bytes 98308
  84.4 22.4 %all-to-all-start.1 = ((f32[128,1,576]{2,1,0:T(1,128)}), f32[128,1,576]{2,1,0:T(1,128)}, u32[]{:S(2)}, u32[]{:S(2)}) async-start(f32[128,1,576]{2,1,0:T(1,128)} %reshape.1816), calls=%async_computation.1 | async-start | bytes 655360 | tf_op jit(solution)/shard_map/all_to_all | solution.py:226
  96.4 20.0 %copy-start.61 = (s32[4096]{0:T(1024)S(1)}, s32[4096]{0:T(1024)}, u32[]{:S(2)}) copy-start(s32[4096]{0:T(1024)} %broadcast_clamp_fusion.1) | copy-start | bytes 49156
  136.7 7.5 %copy-start.23 = (f32[9,32,128]{2,0,1:T(8,128)}, f32[9,32,128]{2,0,1:T(8,128)S(1)}, u32[]{:S(2)}) copy-start(f32[9,32,128]{2,0,1:T(8,128)S(1)} %select_bitcast_fusion.1) | copy-start | bytes 442372
  144.3 8.7 %copy-start = (f32[32,128,256]{2,0,1:T(8,128)}, f32[32,128,256]{2,0,1:T(8,128)S(1)}, u32[]{:S(2)}) copy-start(f32[32,128,256]{2,0,1:T(8,128)S(1)} %fusion.22) | copy-start | bytes 12582916
  160.9 4.6 %collective-permute-start = (f32[2,3,5,256]{3,2,1,0:T(8,128)S(1)}, f32[2,3,5,256]{3,2,1,0:T(8,128)S(1)}, u32[]{:S(2)}, u32[]{:S(2)}) collective-permute-start(f32[2,3,5,256]{3,2,1,0:T(8,128)S(1)} %get-tuple-element.163), channel_id=1, source_target_pairs={{0,16},{16,32},{32,48},{48,64},{64,80},{80,96},{96,112},{1,17},{17... | collective-permute-start | bytes 92168 | tf_op jit(solution)/shard_map/ppermute | solution.py:42
  163.6 5.4 %collective-permute-start.1 = (f32[2,3,5,256]{3,2,1,0:T(8,128)S(1)}, f32[2,3,5,256]{3,2,1,0:T(8,128)S(1)}, u32[]{:S(2)}, u32[]{:S(2)}) collective-permute-start(f32[2,3,5,256]{3,2,1,0:T(8,128)S(1)} %get-tuple-element.164), channel_id=1, source_target_pairs={{16,0},{32,16},{48,32},{64,48},{80,64},{96,80},{112,96},{17,1},{33... | collective-permute-start | bytes 92168 | tf_op jit(solution)/shard_map/ppermute | solution.py:45
  170.0 4.3 %collective-permute-start.2 = (f32[2,3,42,5]{3,2,1,0:T(8,128)S(1)}, f32[2,3,42,5]{3,2,1,0:T(8,128)S(1)}, u32[]{:S(2)}, u32[]{:S(2)}) collective-permute-start(f32[2,3,42,5]{3,2,1,0:T(8,128)S(1)} %get-tuple-element.155), channel_id=1, source_target_pairs={{0,1},{1,2},{2,3},{3,4},{4,5},{5,6},{6,7},{7,8},{8,9},{9,10},{10,1... | collective-permute-start | bytes 15128 | tf_op jit(solution)/shard_map/ppermute | solution.py:42
  172.3 5.9 %collective-permute-start.3 = (f32[2,3,42,5]{3,2,1,0:T(8,128)S(1)}, f32[2,3,42,5]{3,2,1,0:T(8,128)S(1)}, u32[]{:S(2)}, u32[]{:S(2)}) collective-permute-start(f32[2,3,42,5]{3,2,1,0:T(8,128)S(1)} %get-tuple-element.156), channel_id=1, source_target_pairs={{1,0},{2,1},{3,2},{4,3},{5,4},{6,5},{7,6},{8,7},{9,8},{10,9},{11,1... | collective-permute-start | bytes 15128 | tf_op jit(solution)/shard_map/ppermute | solution.py:45
  179.5 18.0 %copy-start.46 = (s32[2,16,128]{2,1,0:T(8,128)S(1)}, s32[2,16,128]{2,1,0:T(8,128)}, u32[]{:S(2)}) copy-start(s32[2,16,128]{2,1,0:T(8,128)} %param.10) | copy-start | bytes 49156
  182.9 13.3 %copy-start.7 = (f32[3,32,256]{2,1,0:T(8,128)}, f32[3,32,256]{2,1,0:T(8,128)S(1)}, u32[]{:S(2)}) copy-start(f32[3,32,256]{2,1,0:T(8,128)S(1)} %get-tuple-element.88) | copy-start | bytes 294916
  183.0 10.3 %copy-start.5 = (f32[3,32,256]{2,1,0:T(8,128)}, f32[3,32,256]{2,1,0:T(8,128)S(1)}, u32[]{:S(2)}) copy-start(f32[3,32,256]{2,1,0:T(8,128)S(1)} %get-tuple-element.149) | copy-start | bytes 294916
  183.0 10.3 %copy-start.6 = (f32[3,32,256]{2,1,0:T(8,128)}, f32[3,32,256]{2,1,0:T(8,128)S(1)}, u32[]{:S(2)}) copy-start(f32[3,32,256]{2,1,0:T(8,128)S(1)} %get-tuple-element.150) | copy-start | bytes 294916
  183.1 5.6 %collective-permute-start.4 = (f32[9,5,256]{2,1,0:T(8,128)S(1)}, f32[9,5,256]{2,1,0:T(8,128)S(1)}, u32[]{:S(2)}, u32[]{:S(2)}) collective-permute-start(f32[9,5,256]{2,1,0:T(8,128)S(1)} %get-tuple-element.153), channel_id=1, source_target_pairs={{0,16},{16,32},{32,48},{48,64},{64,80},{80,96},{96,112},{1,17},{17... | collective-permute-start | bytes 138248 | tf_op jit(solution)/shard_map/ppermute | solution.py:42
  186.7 5.7 %collective-permute-start.5 = (f32[9,5,256]{2,1,0:T(8,128)S(1)}, f32[9,5,256]{2,1,0:T(8,128)S(1)}, u32[]{:S(2)}, u32[]{:S(2)}) collective-permute-start(f32[9,5,256]{2,1,0:T(8,128)S(1)} %get-tuple-element.154), channel_id=1, source_target_pairs={{16,0},{32,16},{48,32},{64,48},{80,64},{96,80},{112,96},{17,1},{33... | collective-permute-start | bytes 138248 | tf_op jit(solution)/shard_map/ppermute | solution.py:45
  188.7 7.5 %copy-start.59 = (f32[9,5,256]{2,1,0:T(8,128)}, f32[9,5,256]{2,1,0:T(8,128)S(1)}, u32[]{:S(2)}) copy-start(f32[9,5,256]{2,1,0:T(8,128)S(1)} %collective-permute-done.4) | copy-start | bytes 138244
  193.3 14.5 %collective-permute-start.6 = (f32[9,42,5]{2,1,0:T(8,128)}, f32[9,42,5]{2,1,0:T(8,128)}, u32[]{:S(2)}, u32[]{:S(2)}) collective-permute-start(f32[9,42,5]{2,1,0:T(8,128)} %get-tuple-element.151), channel_id=1, source_target_pairs={{0,1},{1,2},{2,3},{3,4},{4,5},{5,6},{6,7},{7,8},{8,9},{9,10},{10,1... | collective-permute-start | bytes 22688 | tf_op jit(solution)/shard_map/ppermute | solution.py:42
  196.2 11.6 %collective-permute-start.7 = (f32[9,42,5]{2,1,0:T(8,128)}, f32[9,42,5]{2,1,0:T(8,128)}, u32[]{:S(2)}, u32[]{:S(2)}) collective-permute-start(f32[9,42,5]{2,1,0:T(8,128)} %get-tuple-element.152), channel_id=1, source_target_pairs={{1,0},{2,1},{3,2},{4,3},{5,4},{6,5},{7,6},{8,7},{9,8},{10,9},{11,1... | collective-permute-start | bytes 22688 | tf_op jit(solution)/shard_map/ppermute | solution.py:45
  220.0 10.2 %copy-start.1 = (f32[32,128,256]{2,0,1:T(8,128)S(1)}, f32[32,128,256]{2,0,1:T(8,128)}, u32[]{:S(2)}) copy-start(f32[32,128,256]{2,0,1:T(8,128)} %copy-done) | copy-start | bytes 12582916
  220.0 10.2 %copy-start.24 = (f32[9,32,128]{2,0,1:T(8,128)S(1)}, f32[9,32,128]{2,0,1:T(8,128)}, u32[]{:S(2)}) copy-start(f32[9,32,128]{2,0,1:T(8,128)} %copy-done.23) | copy-start | bytes 442372
  220.0 10.2 %copy-start.36 = (f32[1,32,128]{2,0,1:T(1,128)S(1)}, f32[1,32,128]{2,0,1:T(1,128)}, u32[]{:S(2)}) copy-start(f32[1,32,128]{2,0,1:T(1,128)} %copy-done.35) | copy-start | bytes 49156
  220.0 10.2 %copy-start.38 = (f32[1,32,128]{2,0,1:T(1,128)S(1)}, f32[1,32,128]{2,0,1:T(1,128)}, u32[]{:S(2)}) copy-start(f32[1,32,128]{2,0,1:T(1,128)} %copy-done.37) | copy-start | bytes 49156
  220.0 10.3 %copy-start.40 = (f32[1,32,128]{2,0,1:T(1,128)S(1)}, f32[1,32,128]{2,0,1:T(1,128)}, u32[]{:S(2)}) copy-start(f32[1,32,128]{2,0,1:T(1,128)} %copy-done.39) | copy-start | bytes 49156
  220.0 10.3 %copy-start.42 = (f32[1,32,128]{2,0,1:T(1,128)S(1)}, f32[1,32,128]{2,0,1:T(1,128)}, u32[]{:S(2)}) copy-start(f32[1,32,128]{2,0,1:T(1,128)} %copy-done.41) | copy-start | bytes 49156
  220.1 10.3 %copy-start.44 = (f32[32,128]{1,0:T(8,128)S(1)}, f32[32,128]{1,0:T(8,128)}, u32[]{:S(2)}) copy-start(f32[32,128]{1,0:T(8,128)} %copy-done.43) | copy-start | bytes 49156
  220.1 10.3 %copy-start.58 = (f32[3,32,256]{2,1,0:T(8,128)S(1)}, f32[3,32,256]{2,1,0:T(8,128)}, u32[]{:S(2)}) copy-start(f32[3,32,256]{2,1,0:T(8,128)} %squeeze.314) | copy-start | bytes 294916
  220.1 10.3 %copy-start.63 = (f32[256]{0:T(256)S(1)}, f32[256]{0:T(256)}, u32[]{:S(2)}) copy-start(f32[256]{0:T(256)} %get-tuple-element.236) | copy-start | bytes 3076
  220.1 10.3 %copy-start.65 = (f32[256]{0:T(256)S(1)}, f32[256]{0:T(256)}, u32[]{:S(2)}) copy-start(f32[256]{0:T(256)} %get-tuple-element.237) | copy-start | bytes 3076
  249.7 16.0 %copy-start.66 = (s32[32]{0:T(128)S(1)}, s32[32]{0:T(128)}, u32[]{:S(2)}) copy-start(s32[32]{0:T(128)} %lt.108) | copy-start | bytes 388
  300.7 22.0 %all-to-all-start.2 = ((f32[128,1,576]{2,1,0:T(1,128)}), f32[128,1,576]{2,1,0:T(1,128)}, u32[]{:S(2)}, u32[]{:S(2)}) async-start(f32[128,1,576]{2,1,0:T(1,128)} %reshape.1818), calls=%async_computation.2 | async-start | bytes 655360 | tf_op jit(solution)/shard_map/all_to_all | solution.py:230
  346.0 12.4 %copy-start.8 = (f32[1,128,64]{1,2,0:T(8,128)S(1)}, f32[1,128,64]{1,2,0:T(8,128)}, u32[]{:S(2)}) copy-start(f32[1,128,64]{1,2,0:T(8,128)} %copy.211) | copy-start | bytes 98308
  346.0 14.3 %copy-start.10 = (f32[1,128,64]{1,2,0:T(8,128)S(1)}, f32[1,128,64]{1,2,0:T(8,128)}, u32[]{:S(2)}) copy-start(f32[1,128,64]{1,2,0:T(8,128)} %copy-done.9) | copy-start | bytes 98308
  346.0 14.3 %copy-start.12 = (f32[1,128,64]{1,2,0:T(8,128)S(1)}, f32[1,128,64]{1,2,0:T(8,128)}, u32[]{:S(2)}) copy-start(f32[1,128,64]{1,2,0:T(8,128)} %copy-done.11) | copy-start | bytes 98308
  346.0 14.3 %copy-start.14 = (f32[1,128,64]{1,2,0:T(8,128)S(1)}, f32[1,128,64]{1,2,0:T(8,128)}, u32[]{:S(2)}) copy-start(f32[1,128,64]{1,2,0:T(8,128)} %copy-done.13) | copy-start | bytes 98308
  346.0 14.3 %copy-start.20 = (f32[1,128,64]{1,2,0:T(8,128)S(1)}, f32[1,128,64]{1,2,0:T(8,128)}, u32[]{:S(2)}) copy-start(f32[1,128,64]{1,2,0:T(8,128)} %copy-done.19) | copy-start | bytes 98308
  346.1 14.3 %copy-start.22 = (f32[1,128,64]{1,2,0:T(8,128)S(1)}, f32[1,128,64]{1,2,0:T(8,128)}, u32[]{:S(2)}) copy-start(f32[1,128,64]{1,2,0:T(8,128)} %copy-done.21) | copy-start | bytes 98308
  346.1 14.3 %copy-start.26 = (f32[1,128,64]{1,2,0:T(8,128)S(1)}, f32[1,128,64]{1,2,0:T(8,128)}, u32[]{:S(2)}) copy-start(f32[1,128,64]{1,2,0:T(8,128)} %copy-done.25) | copy-start | bytes 98308
  346.1 14.3 %copy-start.28 = (f32[1,128,64]{1,2,0:T(8,128)S(1)}, f32[1,128,64]{1,2,0:T(8,128)}, u32[]{:S(2)}) copy-start(f32[1,128,64]{1,2,0:T(8,128)} %copy-done.27) | copy-start | bytes 98308
  346.1 14.3 %copy-start.29 = (f32[1,128,64]{1,2,0:T(8,128)S(1)}, f32[1,128,64]{1,2,0:T(8,128)}, u32[]{:S(2)}) copy-start(f32[1,128,64]{1,2,0:T(8,128)} %get-tuple-element.99) | copy-start | bytes 98308
  346.1 14.3 %copy-start.30 = (f32[1,128,64]{1,2,0:T(8,128)S(1)}, f32[1,128,64]{1,2,0:T(8,128)}, u32[]{:S(2)}) copy-start(f32[1,128,64]{1,2,0:T(8,128)} %get-tuple-element.101) | copy-start | bytes 98308
  346.1 14.3 %copy-start.31 = (f32[1,128,64]{1,2,0:T(8,128)S(1)}, f32[1,128,64]{1,2,0:T(8,128)}, u32[]{:S(2)}) copy-start(f32[1,128,64]{1,2,0:T(8,128)} %get-tuple-element.103) | copy-start | bytes 98308
  346.1 14.3 %copy-start.32 = (f32[1,128,64]{1,2,0:T(8,128)S(1)}, f32[1,128,64]{1,2,0:T(8,128)}, u32[]{:S(2)}) copy-start(f32[1,128,64]{1,2,0:T(8,128)} %get-tuple-element.106) | copy-start | bytes 98308
  346.1 14.3 %copy-start.33 = (f32[1,128,64]{1,2,0:T(8,128)S(1)}, f32[1,128,64]{1,2,0:T(8,128)}, u32[]{:S(2)}) copy-start(f32[1,128,64]{1,2,0:T(8,128)} %get-tuple-element.108) | copy-start | bytes 98308
  346.1 14.3 %copy-start.34 = (f32[1,128,64]{1,2,0:T(8,128)S(1)}, f32[1,128,64]{1,2,0:T(8,128)}, u32[]{:S(2)}) copy-start(f32[1,128,64]{1,2,0:T(8,128)} %get-tuple-element.110) | copy-start | bytes 98308
  346.1 14.3 %copy-start.48 = (f32[1,128,64]{1,2,0:T(8,128)S(1)}, f32[1,128,64]{1,2,0:T(8,128)}, u32[]{:S(2)}) copy-start(f32[1,128,64]{1,2,0:T(8,128)} %copy.216) | copy-start | bytes 98308
  346.2 14.3 %copy-start.49 = (f32[1,128,64]{1,2,0:T(8,128)S(1)}, f32[1,128,64]{1,2,0:T(8,128)}, u32[]{:S(2)}) copy-start(f32[1,128,64]{1,2,0:T(8,128)} %copy.215) | copy-start | bytes 98308
  346.2 14.3 %copy-start.50 = (f32[1,128,64]{1,2,0:T(8,128)S(1)}, f32[1,128,64]{1,2,0:T(8,128)}, u32[]{:S(2)}) copy-start(f32[1,128,64]{1,2,0:T(8,128)} %copy.214) | copy-start | bytes 98308
  346.2 14.3 %copy-start.51 = (f32[1,128,64]{1,2,0:T(8,128)S(1)}, f32[1,128,64]{1,2,0:T(8,128)}, u32[]{:S(2)}) copy-start(f32[1,128,64]{1,2,0:T(8,128)} %get-tuple-element.105) | copy-start | bytes 98308
  346.2 18.3 %copy-start.18 = (f32[1,128,64]{1,2,0:T(8,128)S(1)}, f32[1,128,64]{1,2,0:T(8,128)}, u32[]{:S(2)}) copy-start(f32[1,128,64]{1,2,0:T(8,128)} %copy-done.17) | copy-start | bytes 98308
  346.2 22.2 %copy-start.47 = (f32[1,128,64]{1,2,0:T(8,128)S(1)}, f32[1,128,64]{1,2,0:T(8,128)}, u32[]{:S(2)}) copy-start(f32[1,128,64]{1,2,0:T(8,128)} %copy.210) | copy-start | bytes 98308
  346.2 22.2 %copy-start.15 = (f32[1,128,64]{1,2,0:T(8,128)S(1)}, f32[1,128,64]{1,2,0:T(8,128)}, u32[]{:S(2)}) copy-start(f32[1,128,64]{1,2,0:T(8,128)} %copy.213) | copy-start | bytes 98308
  346.2 22.2 %copy-start.16 = (f32[1,128,64]{1,2,0:T(8,128)S(1)}, f32[1,128,64]{1,2,0:T(8,128)}, u32[]{:S(2)}) copy-start(f32[1,128,64]{1,2,0:T(8,128)} %copy.212) | copy-start | bytes 98308
  349.0 19.7 %copy-start.52 = (f32[1,128,64]{1,2,0:T(8,128)S(1)}, f32[1,128,64]{1,2,0:T(8,128)}, u32[]{:S(2)}) copy-start(f32[1,128,64]{1,2,0:T(8,128)} %get-tuple-element.100) | copy-start | bytes 98308
  349.0 19.7 %copy-start.53 = (f32[1,128,64]{1,2,0:T(8,128)S(1)}, f32[1,128,64]{1,2,0:T(8,128)}, u32[]{:S(2)}) copy-start(f32[1,128,64]{1,2,0:T(8,128)} %get-tuple-element.102) | copy-start | bytes 98308
  349.0 19.7 %copy-start.54 = (f32[1,128,64]{1,2,0:T(8,128)S(1)}, f32[1,128,64]{1,2,0:T(8,128)}, u32[]{:S(2)}) copy-start(f32[1,128,64]{1,2,0:T(8,128)} %get-tuple-element.104) | copy-start | bytes 98308
  349.0 19.7 %copy-start.55 = (f32[1,128,64]{1,2,0:T(8,128)S(1)}, f32[1,128,64]{1,2,0:T(8,128)}, u32[]{:S(2)}) copy-start(f32[1,128,64]{1,2,0:T(8,128)} %get-tuple-element.107) | copy-start | bytes 98308
  349.0 19.7 %copy-start.56 = (f32[1,128,64]{1,2,0:T(8,128)S(1)}, f32[1,128,64]{1,2,0:T(8,128)}, u32[]{:S(2)}) copy-start(f32[1,128,64]{1,2,0:T(8,128)} %get-tuple-element.109) | copy-start | bytes 98308
  349.0 19.7 %copy-start.57 = (f32[1,128,64]{1,2,0:T(8,128)S(1)}, f32[1,128,64]{1,2,0:T(8,128)}, u32[]{:S(2)}) copy-start(f32[1,128,64]{1,2,0:T(8,128)} %get-tuple-element.111) | copy-start | bytes 98308
  (14 other events, 69.0 us)
where the time goes:
time: 437 us; the launch traced here: 430 us
  other arithmetic  168 us (38%)
  local copies, waits for them, and re-layouts  135 us (31%)
  starting transfers between devices  50.6 us (12%)
  matrix products  35.1 us (8%)
  waiting for transfers between devices  31.8 us (7%)
  between operations  9.32 us (2%)
    scatter-add x1, other arithmetic, shards(): gradient = jnp.zeros_like(attributes).at[:, received.reshape(-1)].add(row...  46.5 us
    gather x2, local copies, waits for them, and re-layouts, shards(): owner_rows = jnp.take(attributes, received, axis=1)  35.4 us
    dot_general x3, matrix products, render_block(): jnp.einsum('cbk,bkp->cbp', tile_feats[6:9], weight, precision=lax.Precisi...  27.8 us
    unnamed x151, local copies, waits for them, and re-layouts  27.6 us
    scatter-add x1, other arithmetic, shards(): jnp.zeros((feat_count, slots), jnp.float32).at[:, entry_ids]  24.9 us
    gather x2, local copies, waits for them, and re-layouts, shards(): jnp.take(feature_flat, entry_ids, axis=1)  19.3 us
    reduce_sum x1, other arithmetic, render_block(): tile_feats[4][:, :, None] * delta_y * delta_y  16 us
    another operation x2, other arithmetic, render_block(): before = jnp.cumsum(log_keep, axis=1) - log_keep  12.8 us
  transfers between devices with their start and end apart: 11, of which 6 were waited for; matrix products, arithmetic and copies ran while one was open for 4% of the time, Pallas kernels for 0%

commit v1 on v0

v1 whole, which is shorter than its diff:
```python
import math

import jax
import jax.numpy as jnp
from jax import lax
from jax.experimental import pallas as pl
from jax.experimental.pallas import tpu as pltpu
from jax.sharding import PartitionSpec as P

F32 = jnp.float32
BF16 = jnp.bfloat16
I32 = jnp.int32
MESH = pl.DeviceIdType.MESH

TILE = 16
N_IMG = 8
N_CELL = 16
DEVICES = 128
LIST = 128
TILES = 32
ATTRS = 59
ROWS = 64
FEATS = 9
PAIRS = 5

WEIGHT_SSIM = 0.2
SMOOTHING = 0.01
STAB_ONE = 0.0001
STAB_TWO = 0.0009
BLUR_SIGMA = 1.5
SH_ZERO = 0.28209479177387814
SH_ONE = 0.4886025119029199
SH_TWO = (
    1.0925484305920792,
    -1.0925484305920792,
    0.31539156525252005,
    -1.0925484305920792,
    0.5462742152960396,
)
SH_THREE = (
    -0.5900435899266435,
    2.890611442640554,
    -0.4570457994644658,
    0.3731763325901154,
    -0.4570457994644658,
    1.445305721320277,
    -0.5900435899266435,
)


def blur_taps():
    raw = [math.exp(-((o - 5.0) ** 2) / (2.0 * BLUR_SIGMA * BLUR_SIGMA)) for o in range(11)]
    return [r / sum(raw) for r in raw]


TAPS = blur_taps()


def harmonic_basis(ux, uy, uz):
    xx, yy, zz = ux * ux, uy * uy, uz * uz
    return [
        SH_ZERO,
        -SH_ONE * uy,
        SH_ONE * uz,
        -SH_ONE * ux,
        SH_TWO[0] * ux * uy,
        SH_TWO[1] * uy * uz,
        SH_TWO[2] * (2.0 * zz - xx - yy),
        SH_TWO[3] * ux * uz,
        SH_TWO[4] * (xx - yy),
        SH_THREE[0] * uy * (3.0 * xx - yy),
        SH_THREE[1] * ux * uy * uz,
        SH_THREE[2] * uy * (4.0 * zz - xx - yy),
        SH_THREE[3] * uz * (2.0 * zz - 3.0 * xx - 3.0 * yy),
        SH_THREE[4] * ux * (4.0 * zz - xx - yy),
        SH_THREE[5] * uz * (xx - yy),
        SH_THREE[6] * ux * (xx - 3.0 * yy),
    ]


def project(rows, cam):
    pos = rows[0:3]
    scales = [jnp.exp(r) for r in rows[3:6]]
    qw = 1.5 + jnp.tanh(rows[6])
    qx, qy, qz = rows[7:10]
    inv = 1.0 / jnp.sqrt(qw * qw + qx * qx + qy * qy + qz * qz)
    qw, qx, qy, qz = qw * inv, qx * inv, qy * inv, qz * inv
    rot = [
        [1.0 - 2.0 * (qy * qy + qz * qz), 2.0 * (qx * qy - qw * qz), 2.0 * (qx * qz + qw * qy)],
        [2.0 * (qx * qy + qw * qz), 1.0 - 2.0 * (qx * qx + qz * qz), 2.0 * (qy * qz - qw * qx)],
        [2.0 * (qx * qz - qw * qy), 2.0 * (qy * qz + qw * qx), 1.0 - 2.0 * (qx * qx + qy * qy)],
    ]
    axes = [
        [
            (cam[s][0] * rot[0][k] + cam[s][1] * rot[1][k] + cam[s][2] * rot[2][k]) * scales[k]
            for k in range(3)
        ]
        for s in range(2)
    ]
    cov_a = axes[0][0] * axes[0][0] + axes[0][1] * axes[0][1] + axes[0][2] * axes[0][2] + 0.3
    cov_b = axes[0][0] * axes[1][0] + axes[0][1] * axes[1][1] + axes[0][2] * axes[1][2]
    cov_c = axes[1][0] * axes[1][0] + axes[1][1] * axes[1][1] + axes[1][2] * axes[1][2] + 0.3
    inv_det = 1.0 / (cov_a * cov_c - cov_b * cov_b)
    centers = [
        8.0
        + 7.0 * jnp.sin((cam[s][0] * pos[0] + cam[s][1] * pos[1] + cam[s][2] * pos[2]) / 3.0)
        for s in range(2)
    ]
    off = [pos[k] - cam[2][k] for k in range(3)]
    inv_dist = 1.0 / jnp.sqrt(off[0] * off[0] + off[1] * off[1] + off[2] * off[2])
    basis = harmonic_basis(off[0] * inv_dist, off[1] * inv_dist, off[2] * inv_dist)
    colours = []
    for c in range(3):
        total = 0.5 + basis[0] * rows[11 + 16 * c]
        for m in range(1, 16):
            total = total + basis[m] * rows[11 + 16 * c + m]
        colours.append(total)
    return centers + [cov_c * inv_det, -cov_b * inv_det, cov_a * inv_det] + colours


def read_camera(cam):
    return [[cam[s, k] for k in range(3)] for s in range(3)]


def spread_rows(attr, arows):
    def step(ct, carry):
        lanes = pl.ds(pl.multiple_of(ct * 128, 128), 128)
        for g in range(8):
            n = min(8, ATTRS - 8 * g)
            arows[pl.ds(pl.multiple_of(g * 512 + ct * 8, 8), n), :] = attr[8 * g : 8 * g + n, lanes]
        return carry

    lax.fori_loop(0, 64, step, 0)


def attr_rows(h):
    return [pl.ds((r // 8) * 512 + h * 64 + r % 8, 8, stride=8) for r in range(ATTRS)]


def wrap(value, count):
    return jnp.where(value >= count, value - count, value)


def each_peer(img, cell, act):
    for i in range(N_IMG):
        pi = wrap(img + i, N_IMG) if i else img

        def step(j, carry, pi=pi):
            act(pi, wrap(cell + j, N_CELL))
            return carry

        lax.fori_loop(0 if i else 1, N_CELL, step, 0)


def left_half():
    return lax.broadcasted_iota(I32, (8, 128), 1) < 64


def pack_message(values, msg, low_row, high_row):
    left = left_half()
    for i in range(PAIRS):
        a = values[2 * i]
        b = values[2 * i + 1] if 2 * i + 1 < FEATS else a
        msg[low_row(i), :] = jnp.where(left, a, pltpu.roll(b, 64, 1))
        msg[high_row(i), :] = jnp.where(left, pltpu.roll(a, 64, 1), b)


def unpack_message(msg, low_row, high_row):
    left = left_half()
    values = []
    for i in range(PAIRS):
        low, high = msg[low_row(i), :], msg[high_row(i), :]
        values.append(jnp.where(left, low, pltpu.roll(high, 64, 1)))
        if 2 * i + 1 < FEATS:
            values.append(jnp.where(left, pltpu.roll(low, 64, 1), high))
    return values


def lane_gather(table, ids):
    high = [v // 128 for v in ids]
    low = [v - h * 128 for v, h in zip(ids, high)]
    count = len(ids)

    def step(k8, carry):
        carry = list(carry)
        for kk in range(8):
            k = k8 * 8 + kk
            masks = [h == k for h in high]
            for f in range(FEATS):
                row = jnp.broadcast_to(table[pl.ds(f * ROWS + k, 1), :], (8, 128))
                for c in range(count):
                    got = jnp.take_along_axis(row, low[c], axis=1, mode="promise_in_bounds")
                    carry[c * FEATS + f] = jnp.where(masks[c], got, carry[c * FEATS + f])
        return tuple(carry)

    init = tuple(jnp.zeros((8, 128), F32) for _ in range(count * FEATS))
    out = lax.fori_loop(0, 8, step, init)
    return [list(out[c * FEATS : (c + 1) * FEATS]) for c in range(count)]


def scatter_block(ids, grads, acc):
    high = ids // 256
    low = ids - high * 256
    mask = lax.broadcasted_iota(I32, (32, 256), 0) == high
    upper, lower = [], []
    for g in grads:
        top = g.astype(BF16).astype(F32)
        upper.append(jnp.where(mask, top, 0.0).astype(BF16))
        lower.append(jnp.where(mask, g - top, 0.0).astype(BF16))
    lhs = jnp.concatenate(upper + lower, axis=0)
    hot = jnp.where(lax.broadcasted_iota(I32, (256, 256), 0) == low, 1.0, 0.0).astype(BF16)
    acc[...] += lax.dot_general(
        lhs, hot, (((1,), (1,)), ((), ())), preferred_element_type=F32
    )


def two_parts(v):
    top = v.astype(BF16)
    return top, (v - top.astype(F32)).astype(BF16)


def swap_blocks(z):
    rows = z.shape[0]
    row_at = lax.broadcasted_iota(I32, z.shape, 0)
    lane_at = lax.broadcasted_iota(I32, z.shape, 1)
    for bit in (1, 2, 4, 8):
        row_bit = (row_at // bit) % 2
        lane_bit = (lane_at // (16 * bit)) % 2
        down = pltpu.roll(pltpu.roll(z, rows - bit, 0), 16 * bit, 1)
        up = pltpu.roll(pltpu.roll(z, bit, 0), 256 - 16 * bit, 1)
        z = jnp.where(row_bit == lane_bit, z, jnp.where(row_bit == 0, down, up))
    return z


def border_block(lane_tile, row_block):
    return (lane_tile * 4 + row_block) * 48


def border_copies(ext, img, cell, send, recv):
    west, east = jnp.where(cell == 0, N_CELL - 1, cell - 1), wrap(cell + 1, N_CELL)
    north, south = jnp.where(img == 0, N_IMG - 1, img - 1), wrap(img + 1, N_IMG)
    plan = [
        (border_block(1, 1), border_block(3, 1), 96, img, west),
        (border_block(2, 1), border_block(0, 1), 96, img, east),
    ]
    for lane_tile in (1, 2):
        plan.append((border_block(lane_tile, 1), border_block(lane_tile, 3), 48, north, cell))
        plan.append((border_block(lane_tile, 2), border_block(lane_tile, 0), 48, south, cell))
    plan.append((border_block(1, 1), border_block(3, 3), 48, north, west))
    plan.append((border_block(2, 1), border_block(0, 3), 48, north, east))
    plan.append((border_block(1, 2), border_block(3, 0), 48, south, west))
    plan.append((border_block(2, 2), border_block(0, 0), 48, south, east))
    for source, dest, count, to_img, to_cell in plan:
        pltpu.make_async_remote_copy(
            src_ref=ext.at[pl.ds(source, count)],
            dst_ref=ext.at[pl.ds(dest, count)],
            send_sem=send,
            recv_sem=recv,
            device_id=(to_img, to_cell),
            device_id_type=MESH,
        ).start()


BORDER_ROWS = 2 * 96 + 8 * 48


def wait_rows(ref, count, sem):
    part = ref.at[pl.ds(0, count)]
    pltpu.make_async_copy(part, part, sem).wait()


def window(ext, img, cell, c, row_block):
    left = lax.broadcasted_iota(I32, (16, 128), 1) < 64
    tiles = []
    for lane_tile in range(4):
        v = ext[pl.ds(border_block(lane_tile, row_block) + c * 16, 16), :]
        bad = None
        if lane_tile == 0:
            bad = cell == 0
        if lane_tile == 3:
            bad = cell == N_CELL - 1
        if row_block == 0:
            bad = (img == 0) if bad is None else jnp.logical_or(bad, img == 0)
        if row_block == 3:
            bad = (img == N_IMG - 1) if bad is None else jnp.logical_or(bad, img == N_IMG - 1)
        if bad is not None:
            v = v * jnp.where(bad, 0.0, 1.0)
        tiles.append(pltpu.roll(v, 64, 1))
    return [jnp.where(left, tiles[j], tiles[j + 1]) for j in range(3)]


def blur_down(ref, base, first, count):
    out = []
    for j in range(3):
        start, stride = base
        at = start + j * stride + first
        total = TAPS[5] * ref[pl.ds(at + 5, count), :]
        for o in range(5):
            total = total + TAPS[o] * (
                ref[pl.ds(at + o, count), :] + ref[pl.ds(at + 10 - o, count), :]
            )
        out.append(total)
    return jnp.concatenate(out, axis=1)


def blur_along(v):
    total = TAPS[5] * v
    for o in range(5):
        d = 5 - o
        total = total + TAPS[o] * (pltpu.roll(v, d, 1) + pltpu.roll(v, 384 - d, 1))
    return total


def ssim_value(mean_render, mean_target, square_render, square_target, cross_term):
    spread_render = square_render - mean_render * mean_render
    spread_target = square_target - mean_target * mean_target
    covariance = cross_term - mean_render * mean_target
    upper = (2.0 * mean_render * mean_target + STAB_ONE) * (2.0 * covariance + STAB_TWO)
    lower = (mean_render * mean_render + mean_target * mean_target + STAB_ONE) * (
        spread_render + spread_target + STAB_TWO
    )
    return upper / lower


def map_base(m, c):
    return ((m * 3 + c) * 3 * 64, 64)


def step_kernel(
    cam_ref,
    len_ref,
    vis,
    attr,
    target,
    lists,
    out,
    arows,
    table,
    ids_in,
    ids_own,
    msg,
    inbox,
    msg_back,
    inbox_back,
    ext_render,
    ext_target,
    entry,
    tri_before,
    tri_after,
    weights,
    ratio,
    tile_rows,
    moments,
    maps,
    coefs,
    blurred,
    acc,
    sems,
):
    img = lax.axis_index("img")
    cell = lax.axis_index("cell")
    me = img * N_CELL + cell

    barrier = pltpu.get_barrier_semaphore()
    each_peer(
        img,
        cell,
        lambda pi, pc: pl.semaphore_signal(
            barrier, 1, device_id=(pi, pc), device_id_type=MESH
        ),
    )

    for lane_tile in range(2):
        for t in range(2):
            for c in range(3):
                ext_target[pl.ds(border_block(1 + lane_tile, 1 + t) + c * 16, 16), :] = target[
                    c, 16 * t : 16 * t + 16, 128 * lane_tile : 128 * lane_tile + 128
                ]
    spread_rows(attr, arows)

    pl.semaphore_wait(barrier, DEVICES - 1)

    def send_ids(pi, pc):
        p = pi * N_CELL + pc
        pltpu.make_async_remote_copy(
            src_ref=vis.at[pl.ds(p // 2, 1)],
            dst_ref=ids_in.at[pl.ds(me, 1)],
            send_sem=sems.at[0],
            recv_sem=sems.at[1],
            device_id=(pi, pc),
            device_id_type=MESH,
        ).start()

    each_peer(img, cell, send_ids)
    border_copies(ext_target, img, cell, sems.at[2], sems.at[3])
    ids_in[pl.ds(me, 1), :] = vis[pl.ds(me // 2, 1), :]

    cam = read_camera(cam_ref)

    def project_step(h, carry):
        rows = [arows[at, :] for at in attr_rows(h)]
        feats = project(rows, cam)
        feats.insert(5, jax.nn.sigmoid(rows[10]))
        for f in range(FEATS):
            table[pl.ds(pl.multiple_of(f * ROWS + h * 8, 8), 8), :] = feats[f]
        return carry

    lax.fori_loop(0, 8, project_step, 0)

    row_at = lax.broadcasted_iota(I32, (128, 128), 0)
    lane_at = lax.broadcasted_iota(I32, (128, 128), 1)
    before = jnp.where(row_at < lane_at, 1.0, 0.0).astype(BF16)
    after = jnp.where(row_at > lane_at, 1.0, 0.0).astype(BF16)
    for half in range(2):
        tri_before[128 * half : 128 * half + 128, :] = before
        tri_after[128 * half : 128 * half + 128, :] = after

    wait_rows(ids_in, DEVICES - 1, sems.at[1])
    odd = me - (me // 2) * 2
    left = left_half()

    def gather_step(c2, carry):
        ids = []
        for k in range(2):
            first = ids_in[pl.ds(pl.multiple_of(c2 * 16 + k * 8, 8), 8), :]
            second = ids_in[pl.ds(pl.multiple_of(64 + c2 * 16 + k * 8, 8), 8), :]
            even_form = jnp.where(left, first, pltpu.roll(second, 64, 1))
            odd_form = jnp.where(left, pltpu.roll(first, 64, 1), second)
            v = jnp.where(odd == 0, even_form, odd_form)
            ids_own[pl.ds(pl.multiple_of(c2 * 16 + k * 8, 8), 8), :] = v
            ids.append(v)
        got = lane_gather(table, ids)
        for k in range(2):
            at = (c2 * 2 + k) * 64
            pack_message(
                got[k],
                msg,
                lambda i: pl.ds(at + i, 8, stride=8),
                lambda i: pl.ds(512 + at + i, 8, stride=8),
            )
        return carry

    lax.fori_loop(0, 4, gather_step, 0)

    def send_rows(source, dest, send, recv):
        def act(pi, pc):
            p = pi * N_CELL + pc
            pltpu.make_async_remote_copy(
                src_ref=source.at[pl.ds(pl.multiple_of(p * 8, 8), PAIRS)],
                dst_ref=dest.at[pl.ds(pl.multiple_of(me * 8, 8), PAIRS)],
                send_sem=send,
                recv_sem=recv,
                device_id=(pi, pc),
                device_id_type=MESH,
            ).start()

        each_peer(img, cell, act)
        own = pl.ds(pl.multiple_of(me * 8, 8), PAIRS)
        dest[own, :] = source[own, :]

    send_rows(msg, inbox, sems.at[4], sems.at[5])

    wait_rows(ext_target, BORDER_ROWS, sems.at[3])
    for c in range(3):
        for row_block in range(4):
            parts = window(ext_target, img, cell, c, row_block)
            for j in range(3):
                for m, v in ((3, parts[j]), (4, parts[j] * parts[j])):
                    start, stride = map_base(m, c)
                    maps[pl.ds(start + j * stride + row_block * 16, 16), :] = v
    for m in (3, 4):
        for c in range(3):
            blurred[pl.ds(((m - 3) * 3 + c) * 48, 48), :] = blur_along(
                blur_down(maps, map_base(m, c), 6, 48)
            )

    wait_rows(inbox, (DEVICES - 1) * PAIRS, sems.at[5])

    def table_step(h, carry):
        values = unpack_message(
            inbox,
            lambda i: pl.ds(h * 128 + i, 8, stride=16),
            lambda i: pl.ds(h * 128 + 8 + i, 8, stride=16),
        )
        for f in range(FEATS):
            table[pl.ds(pl.multiple_of(f * ROWS + h * 8, 8), 8), :] = values[f]
        return carry

    lax.fori_loop(0, 8, table_step, 0)

    def list_step(c2, carry):
        at = [pl.multiple_of(c2 * 16 + k * 8, 8) for k in range(2)]
        got = lane_gather(table, [lists[pl.ds(a, 8), :] for a in at])
        for k in range(2):
            for f in range(FEATS):
                entry[pl.ds(pl.multiple_of(f * TILES + at[k], 8), 8), :] = got[k][f]
        return carry

    lax.fori_loop(0, 2, list_step, 0)

    def entry_row(f, t):
        return entry[pl.ds(f * TILES + t, 1), :]

    across = lax.broadcasted_iota(I32, (16, 128), 0).astype(F32) + 0.5
    lane_row = lax.broadcasted_iota(I32, (1, 128), 1)

    def image_row(t, c):
        return (t // 16) * 48 + c * 16 + lax.rem(t, 16)

    def render_step(t, carry):
        alive = lane_row < len_ref[t // 16, lax.rem(t, 16)]
        opacity = jnp.where(alive, entry_row(5, t), 0.0)
        dx = across - entry_row(0, t)
        center_y = entry_row(1, t)
        square_x = (-0.5 * entry_row(2, t)) * dx * dx
        mixed = -entry_row(3, t) * dx
        half_y = -0.5 * entry_row(4, t)
        alpha, logs = [], []
        for y in range(16):
            dy = (y + 0.5) - center_y
            alpha.append(opacity * jnp.exp(square_x + dy * (mixed + half_y * dy)))
            logs.append(jnp.log(1.0 - alpha[y]))
        alpha = jnp.concatenate(alpha, axis=0)
        logs = jnp.concatenate(logs, axis=0)
        before = jnp.dot(
            jnp.concatenate(two_parts(logs), axis=1), tri_before[...], preferred_element_type=F32
        )
        ratio[pl.ds(pl.multiple_of(t * 256, 256), 256), :] = alpha * jnp.exp(-logs)
        weight = jnp.concatenate(two_parts(jnp.exp(before) * alpha), axis=1)
        weights[pl.ds(pl.multiple_of(t * 256, 256), 256), :] = weight
        colour = [two_parts(entry_row(6 + c, t)) for c in range(3)]
        lhs = jnp.concatenate(
            [c[part] for part in range(2) for c in colour] + [jnp.zeros((10, 128), BF16)], axis=0
        )
        pixels = lax.dot_general(
            jnp.concatenate([lhs, lhs], axis=1),
            weight,
            (((1,), (1,)), ((), ())),
            preferred_element_type=F32,
        )
        for c in range(3):
            tile_rows[pl.ds(image_row(t, c), 1), :] = pixels[c : c + 1] + pixels[3 + c : 4 + c]
        return carry

    lax.fori_loop(0, TILES, render_step, 0)

    picture = swap_blocks(tile_rows[...])
    for lane_tile in range(2):
        ext_render[pl.ds(border_block(1 + lane_tile, 1), 96), :] = picture[
            :, 128 * lane_tile : 128 * lane_tile + 128
        ]
    border_copies(ext_render, img, cell, sems.at[6], sems.at[7])
    wait_rows(ext_render, BORDER_ROWS, sems.at[7])

    for c in range(3):
        for row_block in range(4):
            parts = window(ext_render, img, cell, c, row_block)
            start, stride = map_base(3, c)
            for j in range(3):
                rows = pl.ds(start + j * stride + row_block * 16, 16)
                v = parts[j]
                for m, value in ((0, v), (1, v * v), (2, v * maps[rows, :])):
                    first, step = map_base(m, c)
                    maps[pl.ds(first + j * step + row_block * 16, 16), :] = value
    row_at = lax.broadcasted_iota(I32, (48, 384), 0) + (img * 32 - 5)
    lane_at = lax.broadcasted_iota(I32, (48, 384), 1) + (cell * 256 - 64)
    inside = (row_at >= 0) & (row_at < N_IMG * 32) & (lane_at >= 0) & (lane_at < N_CELL * 256)
    for c in range(3):
        mean, square, cross = [
            blur_along(blur_down(maps, map_base(m, c), 6, 48)) for m in range(3)
        ]
        mean_target = blurred[pl.ds(c * 48, 48), :]
        square_target = blurred[pl.ds((3 + c) * 48, 48), :]
        similarity, pullback = jax.vjp(
            lambda a, b, d: ssim_value(a, mean_target, b, square_target, d), mean, square, cross
        )
        for m, v in enumerate(pullback(jnp.full((48, 384), -WEIGHT_SSIM, F32))):
            v = jnp.where(inside, v, 0.0)
            for j in range(3):
                coefs[pl.ds(((m * 3 + c) * 3 + j) * 48, 48), :] = v[:, 128 * j : 128 * j + 128]
    for c in range(3):
        back_mean, back_square, back_cross = [
            blur_along(blur_down(coefs, ((m * 3 + c) * 3 * 48, 48), 0, 32))[:, 64:320]
            for m in range(3)
        ]
        for t in range(2):
            rows = slice(16 * t, 16 * t + 16)
            image = jnp.concatenate(
                [
                    ext_render[pl.ds(border_block(1 + k, 1 + t) + c * 16, 16), :]
                    for k in range(2)
                ],
                axis=1,
            )
            wanted = target[c, rows, :]
            difference = image - wanted
            tile_rows[pl.ds(t * 48 + c * 16, 16), :] = (
                (1.0 - WEIGHT_SSIM)
                * difference
                / jnp.sqrt(difference * difference + SMOOTHING * SMOOTHING)
                + back_mean[rows]
                + 2.0 * image * back_square[rows]
                + wanted * back_cross[rows]
            )
    tile_rows[...] = swap_blocks(tile_rows[...])

    def back_step(t, carry):
        pixel_grad = [two_parts(tile_rows[pl.ds(image_row(t, c), 1), :]) for c in range(3)]
        colour = [two_parts(entry_row(6 + c, t)) for c in range(3)]
        tops, lows = [g[0] for g in pixel_grad], [g[1] for g in pixel_grad]
        grad_rows = jnp.concatenate(tops + lows + tops + [jnp.zeros((7, 256), BF16)], axis=0)
        colour_rows = jnp.concatenate(
            [c[0] for c in colour] * 2 + [c[1] for c in colour] + [jnp.zeros((7, 128), BF16)],
            axis=0,
        )
        value = lax.dot_general(
            grad_rows, colour_rows, (((0,), (0,)), ((), ())), preferred_element_type=F32
        )
        weight = weights[pl.ds(pl.multiple_of(t * 256, 256), 256), :]
        gain = value * (weight[:, :128].astype(F32) + weight[:, 128:].astype(F32))
        later = jnp.dot(
            jnp.concatenate(two_parts(gain), axis=1), tri_after[...], preferred_element_type=F32
        )
        pull = gain - ratio[pl.ds(pl.multiple_of(t * 256, 256), 256), :] * later
        dx = across - entry_row(0, t)
        center_y = entry_row(1, t)
        sum_0 = sum_y = sum_yy = None
        for y in range(16):
            dy = (y + 0.5) - center_y
            part = pull[16 * y : 16 * y + 16]
            part_y = part * dy
            part_yy = part_y * dy
            sum_0 = part if y == 0 else sum_0 + part
            sum_y = part_y if y == 0 else sum_y + part_y
            sum_yy = part_yy if y == 0 else sum_yy + part_yy
        sum_x = sum_0 * dx
        found = [sum_0, sum_x, sum_y, sum_x * dx, sum_y * dx, sum_yy]
        for m in range(6):
            moments[pl.ds(m * TILES + t, 1), :] = jnp.sum(found[m], axis=0, keepdims=True)
        mixed = jnp.dot(grad_rows, weight, preferred_element_type=F32)
        for c in range(3):
            both = mixed[c : c + 1] + mixed[3 + c : 4 + c]
            moments[pl.ds((6 + c) * TILES + t, 1), :] = both[:, :128] + both[:, 128:]
        return carry

    lax.fori_loop(0, TILES, back_step, 0)

    feat = [entry[f * TILES : (f + 1) * TILES, :] for f in range(6)]
    mom = [moments[m * TILES : (m + 1) * TILES, :] for m in range(6)]
    entry[0:TILES, :] = feat[2] * mom[1] + feat[3] * mom[2]
    entry[TILES : 2 * TILES, :] = feat[3] * mom[1] + feat[4] * mom[2]
    entry[2 * TILES : 3 * TILES, :] = -0.5 * mom[3]
    entry[3 * TILES : 4 * TILES, :] = -mom[4]
    entry[4 * TILES : 5 * TILES, :] = -0.5 * mom[5]
    entry[5 * TILES : 6 * TILES, :] = mom[0]
    entry[6 * TILES : 9 * TILES, :] = moments[6 * TILES : 9 * TILES, :]

    acc[...] = jnp.zeros_like(acc)

    def slot_step(b, carry):
        def pair(ref, at):
            both = ref[pl.ds(at, 2), :]
            return jnp.concatenate([both[0:1], both[1:2]], axis=1)

        scatter_block(
            pair(lists, b * 2), [pair(entry, f * TILES + b * 2) for f in range(FEATS)], acc
        )
        return carry

    lax.fori_loop(0, TILES // 2, slot_step, 0)

    def total_rows(f, h):
        a = acc[pl.ds(pl.multiple_of(f * 32 + h * 8, 8), 8), :]
        b = acc[pl.ds(pl.multiple_of(288 + f * 32 + h * 8, 8), 8), :]
        return a + b

    def back_pack(h, carry):
        totals = [total_rows(f, h) for f in range(FEATS)]
        for half in range(2):
            pack_message(
                [v[:, 128 * half : 128 * half + 128] for v in totals],
                msg_back,
                lambda i: pl.ds(h * 256 + (2 * half) * 8 + i, 8, stride=32),
                lambda i: pl.ds(h * 256 + (2 * half + 1) * 8 + i, 8, stride=32),
            )
        return carry

    lax.fori_loop(0, 4, back_pack, 0)
    send_rows(msg_back, inbox_back, sems.at[8], sems.at[9])

    acc[...] = jnp.zeros_like(acc)
    wait_rows(inbox_back, (DEVICES - 1) * PAIRS, sems.at[9])

    def owner_unpack(c, carry):
        values = unpack_message(
            inbox_back,
            lambda i: pl.ds(c * 64 + i, 8, stride=8),
            lambda i: pl.ds(512 + c * 64 + i, 8, stride=8),
        )
        for f in range(FEATS):
            table[pl.ds(pl.multiple_of(f * ROWS + c * 8, 8), 8), :] = values[f]
        return carry

    lax.fori_loop(0, 8, owner_unpack, 0)

    def owner_step(b, carry):
        def pair(ref, at):
            both = ref[pl.ds(at, 2), :]
            return jnp.concatenate([both[0:1], both[1:2]], axis=1)

        scatter_block(
            pair(ids_own, b * 2), [pair(table, f * ROWS + b * 2) for f in range(FEATS)], acc
        )
        return carry

    lax.fori_loop(0, ROWS // 2, owner_step, 0)

    def finish(h, carry):
        for f in range(FEATS):
            v = total_rows(f, h)
            for half in range(2):
                out[pl.ds(f * ROWS + h * 16 + half, 8, stride=2), :] = v[
                    :, 128 * half : 128 * half + 128
                ]
        return carry

    lax.fori_loop(0, 4, finish, 0)

    wait_rows(ids_in, DEVICES - 1, sems.at[0])
    wait_rows(ext_target, BORDER_ROWS, sems.at[2])
    wait_rows(msg, (DEVICES - 1) * PAIRS, sems.at[4])
    wait_rows(ext_render, BORDER_ROWS, sems.at[6])
    wait_rows(msg_back, (DEVICES - 1) * PAIRS, sems.at[8])


def pullback_kernel(cam_ref, attr, feat_grad, out, arows):
    cam = read_camera(cam_ref)
    spread_rows(attr, arows)

    def step(h, carry):
        places = attr_rows(h)
        rows = [arows[at, :] for at in places]
        _, pullback = jax.vjp(lambda r: project(r, cam), rows)
        grads = [
            feat_grad[pl.ds(pl.multiple_of(f * ROWS + h * 8, 8), 8), :] for f in range(FEATS)
        ]
        log_opacity = grads.pop(5)
        (result,) = pullback(grads)
        result[10] = log_opacity * (1.0 - jax.nn.sigmoid(rows[10]))
        for at, v in zip(places, result):
            arows[at, :] = v
        return carry

    lax.fori_loop(0, 8, step, 0)

    def gather_rows(ct, carry):
        lanes = pl.ds(pl.multiple_of(ct * 128, 128), 128)
        for g in range(8):
            n = min(8, ATTRS - 8 * g)
            out[8 * g : 8 * g + n, lanes] = arows[pl.ds(pl.multiple_of(g * 512 + ct * 8, 8), n), :]
        return carry

    lax.fori_loop(0, 64, gather_rows, 0)


def shards(attributes, camera, target, visible_index, tile_lists, tile_len):
    vmem = pl.BlockSpec(memory_space=pltpu.VMEM)
    smem = pl.BlockSpec(memory_space=pltpu.SMEM)
    feat_grad = pl.pallas_call(
        step_kernel,
        out_shape=jax.ShapeDtypeStruct((FEATS * ROWS, 128), F32),
        in_specs=[smem, smem, vmem, vmem, vmem, vmem],
        out_specs=vmem,
        scratch_shapes=[
            pltpu.VMEM((4096, 128), F32),
            pltpu.VMEM((FEATS * ROWS, 128), F32),
            pltpu.VMEM((DEVICES, 128), I32),
            pltpu.VMEM((ROWS, 128), I32),
            pltpu.VMEM((DEVICES * 8, 128), F32),
            pltpu.VMEM((DEVICES * 8, 128), F32),
            pltpu.VMEM((DEVICES * 8, 128), F32),
            pltpu.VMEM((DEVICES * 8, 128), F32),
            pltpu.VMEM((16 * 48, 128), F32),
            pltpu.VMEM((16 * 48, 128), F32),
            pltpu.VMEM((FEATS * TILES, 128), F32),
            pltpu.VMEM((256, 128), BF16),
            pltpu.VMEM((256, 128), BF16),
            pltpu.VMEM((TILES * 256, 256), BF16),
            pltpu.VMEM((TILES * 256, 128), F32),
            pltpu.VMEM((96, 256), F32),
            pltpu.VMEM((FEATS * TILES, 128), F32),
            pltpu.VMEM((5 * 3 * 3 * 64, 128), F32),
            pltpu.VMEM((3 * 3 * 3 * 48, 128), F32),
            pltpu.VMEM((2 * 3 * 48, 384), F32),
            pltpu.VMEM((2 * FEATS * 32, 256), F32),
            pltpu.SemaphoreType.DMA((10,)),
        ],
        compiler_params=pltpu.CompilerParams(
            collective_id=0, has_side_effects=True, vmem_limit_bytes=56 * 1024 * 1024
        ),
        name="splat_step",
    )(
        camera,
        tile_len,
        visible_index.reshape(ROWS, 128),
        attributes,
        target,
        tile_lists.reshape(TILES, LIST),
    )
    return pl.pallas_call(
        pullback_kernel,
        out_shape=jax.ShapeDtypeStruct(attributes.shape, F32),
        in_specs=[smem, vmem, vmem],
        out_specs=vmem,
        scratch_shapes=[pltpu.VMEM((4096, 128), F32)],
        name="splat_pullback",
    )(camera, attributes, feat_grad)


def solution(mesh):
    return jax.shard_map(
        shards,
        mesh=mesh,
        in_specs=(
            P(None, ("img", "cell")),
            P(),
            P(None, "img", "cell"),
            P(("img", "cell"), None),
            P("img", "cell", None),
            P("img", "cell"),
        ),
        out_specs=P(None, ("img", "cell")),
        check_vma=False,
    )
```

time: 437 us -> 103 us (0.24); the launches traced: 430 us -> 103 us
  other arithmetic: 168 us -> 0 us
  local copies, waits for them, and re-layouts: 135 us -> 0 us
  Pallas kernels: 0 us -> 103 us
  starting transfers between devices: 50.6 us -> 0 us
  matrix products: 35.1 us -> 0 us
  waiting for transfers between devices: 31.8 us -> 0 us
  between operations: 9.32 us -> 0.01 us
    pallas_call x0 -> x2, Pallas kernels: none -> 103 us  [the longest x1 97.2 us: shards(): pl.pallas_call(step_kernel, out_shape=jax.ShapeDtypeStruct((FEATS * ROWS,...]
    scatter-add x2 -> x0, other arithmetic: 71.4 us -> none  [the longest x1 46.5 us: shards(): gradient = jnp.zeros_like(attributes).at[:, received.reshape(-1)].add(row...]
    gather x4 -> x0, local copies, waits for them, and re-layouts: 54.7 us -> none  [the longest x2 35.4 us: shards(): owner_rows = jnp.take(attributes, received, axis=1)]
    dot_general x7 -> x0, matrix products: 35.1 us -> none  [the longest x3 27.8 us: render_block(): jnp.einsum('cbk,bkp->cbp', tile_feats[6:9], weight, precision=lax.Precisi...]
    all_to_all x3 -> x0, starting transfers between devices: 32.7 us -> none  [the longest x1 11.5 us: route_requests(): lax.all_to_all(payload, ('img', 'cell'), split_axis=1, concat_axis=1, til...]
    unnamed x151 -> x0, local copies, waits for them, and re-layouts: 27.6 us -> none
    all_to_all x3 -> x0, waiting for transfers between devices: 20.6 us -> none  [the longest x1 10.4 us: route_replies(): lax.all_to_all(payload, ('img', 'cell'), split_axis=1, concat_axis=1, til...]
    add_any x10 -> x0, other arithmetic: 19 us -> none  [the longest x3 9.34 us: project_rows(): camera[screen_axis, world_axis] * positions[world_axis]]
  transfers between devices with their start and end apart: 11 -> 0, of which waited for: 6 -> 0; matrix products, arithmetic and copies ran while one was open for 4% -> 0% of each run, Pallas kernels for 0% -> 0%
where the time goes in v1:
time: 103 us
  Pallas kernels  103 us (100%)
    pallas_call x1, Pallas kernels, shards(): pl.pallas_call(step_kernel, out_shape=jax.ShapeDtypeStruct((FEATS * ROWS,...  97.2 us
    pallas_call x1, Pallas kernels, shards(): pl.pallas_call(pullback_kernel, out_shape=jax.ShapeDtypeStruct(attributes...  5.44 us

profile of v1, /device:TPU:1, one launch (start us, length us, event | category | flops | bytes accessed | tf_op | source)
XLA Modules:
  0.0 102.7 jit_solution(4479911139098596339)
XLA Ops:
  0.0 97.2 %splat_step.1.feat_grad = f32[576,128]{1,0:T(8,128)} custom-call(f32[3,3]{1,0:T(4,128)} %cam_ref.3, s32[2,16]{1,0:T(2,128)} %len_ref.1, s32[64,128]{1,0:T(8,128)} %bitcast.2, f32[59,8192]{1,0:T(8,128)} %attr.3, f32[3,32,256]{2,1,0:T(8,128)} %target.1, s32[32,128]{1,0:T(8,128)} %bitcast.3), custom_call_target="tpu_custom_call" | custom-call | tf_op jit(solution)/shard_map/splat_step/pallas_call | solution.py:769
  97.3 5.4 %splat_pullback.1 = f32[59,8192]{1,0:T(8,128)} custom-call(f32[3,3]{1,0:T(4,128)} %cam_ref.3, f32[59,8192]{1,0:T(8,128)} %attr.3, f32[576,128]{1,0:T(8,128)} %splat_step.1.feat_grad), custom_call_target="tpu_custom_call" | custom-call | tf_op jit(solution)/shard_map/splat_pullback/pallas_call | solution.py:810

commit v2 on v1

--- a/solution.py
+++ b/solution.py
@@ -22,6 +22,7 @@
 ROWS = 64
 FEATS = 9
 PAIRS = 5
+GROUP = 4
 
 WEIGHT_SSIM = 0.2
 SMOOTHING = 0.01
@@ -176,41 +177,68 @@
     return values
 
 
-def lane_gather(table, ids):
-    high = [v // 128 for v in ids]
-    low = [v - h * 128 for v, h in zip(ids, high)]
-    count = len(ids)
-
-    def step(k8, carry):
-        carry = list(carry)
-        for kk in range(8):
-            k = k8 * 8 + kk
-            masks = [h == k for h in high]
-            for f in range(FEATS):
-                row = jnp.broadcast_to(table[pl.ds(f * ROWS + k, 1), :], (8, 128))
-                for c in range(count):
-                    got = jnp.take_along_axis(row, low[c], axis=1, mode="promise_in_bounds")
-                    carry[c * FEATS + f] = jnp.where(masks[c], got, carry[c * FEATS + f])
-        return tuple(carry)
-
-    init = tuple(jnp.zeros((8, 128), F32) for _ in range(count * FEATS))
-    out = lax.fori_loop(0, 8, step, init)
-    return [list(out[c * FEATS : (c + 1) * FEATS]) for c in range(count)]
-
-
-def scatter_block(ids, grads, acc):
-    high = ids // 256
-    low = ids - high * 256
-    mask = lax.broadcasted_iota(I32, (32, 256), 0) == high
-    upper, lower = [], []
-    for g in grads:
-        top = g.astype(BF16).astype(F32)
-        upper.append(jnp.where(mask, top, 0.0).astype(BF16))
-        lower.append(jnp.where(mask, g - top, 0.0).astype(BF16))
-    lhs = jnp.concatenate(upper + lower, axis=0)
-    hot = jnp.where(lax.broadcasted_iota(I32, (256, 256), 0) == low, 1.0, 0.0).astype(BF16)
+def one_hot(low):
+    return jnp.where(lax.broadcasted_iota(I32, (256, 256), 0) == low, 1.0, 0.0).astype(BF16)
+
+
+def split_ids(ids):
+    high = lax.shift_right_logical(ids, 8)
+    return high, ids - lax.shift_left(high, 8)
+
+
+def row_pair(ref, at):
+    both = ref[pl.ds(at, 2), :]
+    return jnp.concatenate([both[0:1], both[1:2]], axis=1)
+
+
+def make_parts(table, parts):
+    for f in range(FEATS):
+        for half in range(2):
+            v = table[pl.ds(f * ROWS + half, 32, stride=2), :]
+            for part in range(3):
+                top = v.astype(BF16)
+                parts[
+                    32 * f : 32 * f + 32, 256 * part + 128 * half : 256 * part + 128 * half + 128
+                ] = top
+                v = v - top.astype(F32)
+
+
+def gather_blocks(parts, ids, hots):
+    found = [
+        jnp.dot(
+            parts[...], jnp.concatenate([hot] * 3, axis=0), preferred_element_type=F32
+        )
+        for hot in hots
+    ]
+    out = []
+    for v, block in zip(found, ids):
+        mask = lax.broadcasted_iota(I32, (32, 256), 0) == split_ids(block)[0]
+        out.append(
+            [
+                jnp.sum(
+                    jnp.where(mask, v[32 * f : 32 * f + 32], 0.0), axis=0, keepdims=True
+                )
+                for f in range(FEATS)
+            ]
+        )
+    return out
+
+
+def scatter_blocks(ids, grads, hots, acc):
+    lhs = []
+    for block, rows in zip(ids, grads):
+        mask = lax.broadcasted_iota(I32, (32, 256), 0) == split_ids(block)[0]
+        upper, lower = [], []
+        for g in rows:
+            top = g.astype(BF16).astype(F32)
+            upper.append(jnp.where(mask, top, 0.0).astype(BF16))
+            lower.append(jnp.where(mask, g - top, 0.0).astype(BF16))
+        lhs.append(jnp.concatenate(upper + lower, axis=0))
     acc[...] += lax.dot_general(
-        lhs, hot, (((1,), (1,)), ((), ())), preferred_element_type=F32
+        jnp.concatenate(lhs, axis=1),
+        hots,
+        (((1,), (1,)), ((), ())),
+        preferred_element_type=F32,
     )
 
 
@@ -330,12 +358,16 @@
     cam_ref,
     len_ref,
     vis,
-    attr,
+    attr_hbm,
     target,
     lists,
     out,
+    attr,
     arows,
     table,
+    parts,
+    hot_list,
+    hot_own,
     ids_in,
     ids_own,
     msg,
@@ -369,6 +401,8 @@
             barrier, 1, device_id=(pi, pc), device_id_type=MESH
         ),
     )
+    load_attr = pltpu.make_async_copy(attr_hbm, attr, sems.at[10])
+    load_attr.start()
 
     for lane_tile in range(2):
         for t in range(2):
@@ -376,7 +410,37 @@
                 ext_target[pl.ds(border_block(1 + lane_tile, 1 + t) + c * 16, 16), :] = target[
                     c, 16 * t : 16 * t + 16, 128 * lane_tile : 128 * lane_tile + 128
                 ]
+
+    def list_hot(b, carry):
+        hot_list[:, pl.ds(pl.multiple_of(b * 256, 256), 256)] = one_hot(
+            split_ids(row_pair(lists, b * 2))[1]
+        )
+        return carry
+
+    lax.fori_loop(0, TILES // 2, list_hot, 0)
+
+    cam = read_camera(cam_ref)
+    load_attr.wait()
     spread_rows(attr, arows)
+
+    def project_step(h, carry):
+        rows = [arows[at, :] for at in attr_rows(h)]
+        feats = project(rows, cam)
+        feats.insert(5, jax.nn.sigmoid(rows[10]))
+        for f in range(FEATS):
+            table[pl.ds(pl.multiple_of(f * ROWS + h * 8, 8), 8), :] = feats[f]
+        return carry
+
+    lax.fori_loop(0, 8, project_step, 0)
+    make_parts(table, parts)
+
+    row_at = lax.broadcasted_iota(I32, (128, 128), 0)
+    lane_at = lax.broadcasted_iota(I32, (128, 128), 1)
+    before = jnp.where(row_at < lane_at, 1.0, 0.0).astype(BF16)
+    after = jnp.where(row_at > lane_at, 1.0, 0.0).astype(BF16)
+    for half in range(2):
+        tri_before[128 * half : 128 * half + 128, :] = before
+        tri_after[128 * half : 128 * half + 128, :] = after
 
     pl.semaphore_wait(barrier, DEVICES - 1)
 
@@ -395,77 +459,12 @@
     border_copies(ext_target, img, cell, sems.at[2], sems.at[3])
     ids_in[pl.ds(me, 1), :] = vis[pl.ds(me // 2, 1), :]
 
-    cam = read_camera(cam_ref)
-
-    def project_step(h, carry):
-        rows = [arows[at, :] for at in attr_rows(h)]
-        feats = project(rows, cam)
-        feats.insert(5, jax.nn.sigmoid(rows[10]))
-        for f in range(FEATS):
-            table[pl.ds(pl.multiple_of(f * ROWS + h * 8, 8), 8), :] = feats[f]
-        return carry
-
-    lax.fori_loop(0, 8, project_step, 0)
-
-    row_at = lax.broadcasted_iota(I32, (128, 128), 0)
-    lane_at = lax.broadcasted_iota(I32, (128, 128), 1)
-    before = jnp.where(row_at < lane_at, 1.0, 0.0).astype(BF16)
-    after = jnp.where(row_at > lane_at, 1.0, 0.0).astype(BF16)
-    for half in range(2):
-        tri_before[128 * half : 128 * half + 128, :] = before
-        tri_after[128 * half : 128 * half + 128, :] = after
-
-    wait_rows(ids_in, DEVICES - 1, sems.at[1])
-    odd = me - (me // 2) * 2
-    left = left_half()
-
-    def gather_step(c2, carry):
-        ids = []
-        for k in range(2):
-            first = ids_in[pl.ds(pl.multiple_of(c2 * 16 + k * 8, 8), 8), :]
-            second = ids_in[pl.ds(pl.multiple_of(64 + c2 * 16 + k * 8, 8), 8), :]
-            even_form = jnp.where(left, first, pltpu.roll(second, 64, 1))
-            odd_form = jnp.where(left, pltpu.roll(first, 64, 1), second)
-            v = jnp.where(odd == 0, even_form, odd_form)
-            ids_own[pl.ds(pl.multiple_of(c2 * 16 + k * 8, 8), 8), :] = v
-            ids.append(v)
-        got = lane_gather(table, ids)
-        for k in range(2):
-            at = (c2 * 2 + k) * 64
-            pack_message(
-                got[k],
-                msg,
-                lambda i: pl.ds(at + i, 8, stride=8),
-                lambda i: pl.ds(512 + at + i, 8, stride=8),
-            )
-        return carry
-
-    lax.fori_loop(0, 4, gather_step, 0)
-
-    def send_rows(source, dest, send, recv):
-        def act(pi, pc):
-            p = pi * N_CELL + pc
-            pltpu.make_async_remote_copy(
-                src_ref=source.at[pl.ds(pl.multiple_of(p * 8, 8), PAIRS)],
-                dst_ref=dest.at[pl.ds(pl.multiple_of(me * 8, 8), PAIRS)],
-                send_sem=send,
-                recv_sem=recv,
-                device_id=(pi, pc),
-                device_id_type=MESH,
-            ).start()
-
-        each_peer(img, cell, act)
-        own = pl.ds(pl.multiple_of(me * 8, 8), PAIRS)
-        dest[own, :] = source[own, :]
-
-    send_rows(msg, inbox, sems.at[4], sems.at[5])
-
     wait_rows(ext_target, BORDER_ROWS, sems.at[3])
     for c in range(3):
         for row_block in range(4):
-            parts = window(ext_target, img, cell, c, row_block)
+            strips = window(ext_target, img, cell, c, row_block)
             for j in range(3):
-                for m, v in ((3, parts[j]), (4, parts[j] * parts[j])):
+                for m, v in ((3, strips[j]), (4, strips[j] * strips[j])):
                     start, stride = map_base(m, c)
                     maps[pl.ds(start + j * stride + row_block * 16, 16), :] = v
     for m in (3, 4):
@@ -473,6 +472,68 @@
             blurred[pl.ds(((m - 3) * 3 + c) * 48, 48), :] = blur_along(
                 blur_down(maps, map_base(m, c), 6, 48)
             )
+
+    wait_rows(ids_in, DEVICES - 1, sems.at[1])
+    odd = me - (me // 2) * 2
+    left = left_half()
+    for c in range(8):
+        first = ids_in[8 * c : 8 * c + 8, :]
+        second = ids_in[64 + 8 * c : 72 + 8 * c, :]
+        even_form = jnp.where(left, first, pltpu.roll(second, 64, 1))
+        odd_form = jnp.where(left, pltpu.roll(first, 64, 1), second)
+        ids_own[8 * c : 8 * c + 8, :] = jnp.where(odd == 0, even_form, odd_form)
+
+    def send_message(source, dest, send, recv, pi, pc):
+        pltpu.make_async_remote_copy(
+            src_ref=source.at[pl.ds(pl.multiple_of((pi * N_CELL + pc) * 8, 8), PAIRS)],
+            dst_ref=dest.at[pl.ds(pl.multiple_of(me * 8, 8), PAIRS)],
+            send_sem=send,
+            recv_sem=recv,
+            device_id=(pi, pc),
+            device_id_type=MESH,
+        ).start()
+
+    left_row = lax.broadcasted_iota(I32, (1, 128), 1) < 64
+    half_img = img - (img // 4) * 4
+    own_group = half_img * 2 + cell // 8
+
+    def reply_step(k, carry):
+        g = wrap(own_group + 1 + k, 8)
+        ids = [row_pair(ids_own, g * 8 + 2 * n) for n in range(4)]
+        hots = [one_hot(split_ids(v)[1]) for v in ids]
+        for n in range(4):
+            hot_own[:, pl.ds(pl.multiple_of(g * 1024 + n * 256, 256), 256)] = hots[n]
+        got = gather_blocks(parts, ids, hots)
+        for n in range(4):
+            for row in range(2):
+                d = g * 8 + 2 * n + row
+                for i in range(PAIRS):
+                    first = got[n][2 * i][:, 128 * row : 128 * row + 128]
+                    second = got[n][min(2 * i + 1, FEATS - 1)][:, 128 * row : 128 * row + 128]
+                    msg[pl.ds(d * 8 + i, 1), :] = jnp.where(
+                        left_row, first, pltpu.roll(second, 64, 1)
+                    )
+                    msg[pl.ds(512 + d * 8 + i, 1), :] = jnp.where(
+                        left_row, pltpu.roll(first, 64, 1), second
+                    )
+        for side in range(2):
+            to_img = 4 * side + g // 2
+
+            def send_step(n, carry):
+                to_cell = (g - (g // 2) * 2) * 8 + n
+
+                @pl.when(jnp.logical_or(to_img != img, to_cell != cell))
+                def _():
+                    send_message(msg, inbox, sems.at[4], sems.at[5], to_img, to_cell)
+
+                return carry
+
+            lax.fori_loop(0, 8, send_step, 0)
+        return carry
+
+    lax.fori_loop(0, 8, reply_step, 0)
+    own = pl.ds(pl.multiple_of(me * 8, 8), PAIRS)
+    inbox[own, :] = msg[own, :]
 
     wait_rows(inbox, (DEVICES - 1) * PAIRS, sems.at[5])
 
@@ -487,16 +548,26 @@
         return carry
 
     lax.fori_loop(0, 8, table_step, 0)
-
-    def list_step(c2, carry):
-        at = [pl.multiple_of(c2 * 16 + k * 8, 8) for k in range(2)]
-        got = lane_gather(table, [lists[pl.ds(a, 8), :] for a in at])
-        for k in range(2):
-            for f in range(FEATS):
-                entry[pl.ds(pl.multiple_of(f * TILES + at[k], 8), 8), :] = got[k][f]
-        return carry
-
-    lax.fori_loop(0, 2, list_step, 0)
+    make_parts(table, parts)
+
+    def list_step(k, carry):
+        got = gather_blocks(
+            parts,
+            [row_pair(lists, k * 8 + 2 * n) for n in range(4)],
+            [
+                hot_list[:, pl.ds(pl.multiple_of(k * 1024 + n * 256, 256), 256)]
+                for n in range(4)
+            ],
+        )
+        for n in range(4):
+            for row in range(2):
+                for f in range(FEATS):
+                    entry[pl.ds(f * TILES + k * 8 + 2 * n + row, 1), :] = got[n][f][
+                        :, 128 * row : 128 * row + 128
+                    ]
+        return carry
+
+    lax.fori_loop(0, 4, list_step, 0)
 
     def entry_row(f, t):
         return entry[pl.ds(f * TILES + t, 1), :]
@@ -504,45 +575,65 @@
     across = lax.broadcasted_iota(I32, (16, 128), 0).astype(F32) + 0.5
     lane_row = lax.broadcasted_iota(I32, (1, 128), 1)
 
-    def image_row(t, c):
-        return (t // 16) * 48 + c * 16 + lax.rem(t, 16)
-
-    def render_step(t, carry):
-        alive = lane_row < len_ref[t // 16, lax.rem(t, 16)]
-        opacity = jnp.where(alive, entry_row(5, t), 0.0)
-        dx = across - entry_row(0, t)
-        center_y = entry_row(1, t)
-        square_x = (-0.5 * entry_row(2, t)) * dx * dx
-        mixed = -entry_row(3, t) * dx
-        half_y = -0.5 * entry_row(4, t)
-        alpha, logs = [], []
-        for y in range(16):
-            dy = (y + 0.5) - center_y
-            alpha.append(opacity * jnp.exp(square_x + dy * (mixed + half_y * dy)))
-            logs.append(jnp.log(1.0 - alpha[y]))
-        alpha = jnp.concatenate(alpha, axis=0)
-        logs = jnp.concatenate(logs, axis=0)
-        before = jnp.dot(
-            jnp.concatenate(two_parts(logs), axis=1), tri_before[...], preferred_element_type=F32
-        )
-        ratio[pl.ds(pl.multiple_of(t * 256, 256), 256), :] = alpha * jnp.exp(-logs)
-        weight = jnp.concatenate(two_parts(jnp.exp(before) * alpha), axis=1)
-        weights[pl.ds(pl.multiple_of(t * 256, 256), 256), :] = weight
-        colour = [two_parts(entry_row(6 + c, t)) for c in range(3)]
-        lhs = jnp.concatenate(
-            [c[part] for part in range(2) for c in colour] + [jnp.zeros((10, 128), BF16)], axis=0
-        )
-        pixels = lax.dot_general(
-            jnp.concatenate([lhs, lhs], axis=1),
-            weight,
-            (((1,), (1,)), ((), ())),
-            preferred_element_type=F32,
-        )
-        for c in range(3):
-            tile_rows[pl.ds(image_row(t, c), 1), :] = pixels[c : c + 1] + pixels[3 + c : 4 + c]
-        return carry
-
-    lax.fori_loop(0, TILES, render_step, 0)
+    def spans(tile_row, k):
+        return [tile_row * 16 + k * GROUP + n for n in range(GROUP)]
+
+    def pixels_of(t):
+        return pl.ds(pl.multiple_of(t * 256, 256), 256)
+
+    for tile_row in range(2):
+
+        def render_step(k, carry, tile_row=tile_row):
+            tiles = spans(tile_row, k)
+            alphas, sums = [], []
+            for n, t in enumerate(tiles):
+                alive = lane_row < len_ref[tile_row, k * GROUP + n]
+                opacity = jnp.where(alive, entry_row(5, t), 0.0)
+                dx = across - entry_row(0, t)
+                center_y = entry_row(1, t)
+                square_x = (-0.5 * entry_row(2, t)) * dx * dx
+                mixed = -entry_row(3, t) * dx
+                half_y = -0.5 * entry_row(4, t)
+                alpha = []
+                for y in range(16):
+                    dy = (y + 0.5) - center_y
+                    alpha.append(opacity * jnp.exp(square_x + dy * (mixed + half_y * dy)))
+                alpha = jnp.concatenate(alpha, axis=0)
+                logs = jnp.log(1.0 - alpha)
+                sums.append(
+                    jnp.dot(
+                        jnp.concatenate(two_parts(logs), axis=1),
+                        tri_before[...],
+                        preferred_element_type=F32,
+                    )
+                )
+                ratio[pixels_of(t), :] = alpha * jnp.exp(-logs)
+                alphas.append(alpha)
+            products = []
+            for n, t in enumerate(tiles):
+                weight = jnp.concatenate(two_parts(jnp.exp(sums[n]) * alphas[n]), axis=1)
+                weights[pixels_of(t), :] = weight
+                colour = [two_parts(entry_row(6 + c, t)) for c in range(3)]
+                lhs = jnp.concatenate(
+                    [c[part] for part in range(2) for c in colour] + [jnp.zeros((10, 128), BF16)],
+                    axis=0,
+                )
+                products.append(
+                    lax.dot_general(
+                        jnp.concatenate([lhs, lhs], axis=1),
+                        weight,
+                        (((1,), (1,)), ((), ())),
+                        preferred_element_type=F32,
+                    )
+                )
+            for n in range(GROUP):
+                for c in range(3):
+                    tile_rows[pl.ds(tile_row * 48 + c * 16 + k * GROUP + n, 1), :] = (
+                        products[n][c : c + 1] + products[n][3 + c : 4 + c]
+                    )
+            return carry
+
+        lax.fori_loop(0, 16 // GROUP, render_step, 0)
 
     picture = swap_blocks(tile_rows[...])
     for lane_tile in range(2):
@@ -604,46 +695,73 @@
             )
     tile_rows[...] = swap_blocks(tile_rows[...])
 
-    def back_step(t, carry):
-        pixel_grad = [two_parts(tile_rows[pl.ds(image_row(t, c), 1), :]) for c in range(3)]
-        colour = [two_parts(entry_row(6 + c, t)) for c in range(3)]
-        tops, lows = [g[0] for g in pixel_grad], [g[1] for g in pixel_grad]
-        grad_rows = jnp.concatenate(tops + lows + tops + [jnp.zeros((7, 256), BF16)], axis=0)
-        colour_rows = jnp.concatenate(
-            [c[0] for c in colour] * 2 + [c[1] for c in colour] + [jnp.zeros((7, 128), BF16)],
-            axis=0,
-        )
-        value = lax.dot_general(
-            grad_rows, colour_rows, (((0,), (0,)), ((), ())), preferred_element_type=F32
-        )
-        weight = weights[pl.ds(pl.multiple_of(t * 256, 256), 256), :]
-        gain = value * (weight[:, :128].astype(F32) + weight[:, 128:].astype(F32))
-        later = jnp.dot(
-            jnp.concatenate(two_parts(gain), axis=1), tri_after[...], preferred_element_type=F32
-        )
-        pull = gain - ratio[pl.ds(pl.multiple_of(t * 256, 256), 256), :] * later
-        dx = across - entry_row(0, t)
-        center_y = entry_row(1, t)
-        sum_0 = sum_y = sum_yy = None
-        for y in range(16):
-            dy = (y + 0.5) - center_y
-            part = pull[16 * y : 16 * y + 16]
-            part_y = part * dy
-            part_yy = part_y * dy
-            sum_0 = part if y == 0 else sum_0 + part
-            sum_y = part_y if y == 0 else sum_y + part_y
-            sum_yy = part_yy if y == 0 else sum_yy + part_yy
-        sum_x = sum_0 * dx
-        found = [sum_0, sum_x, sum_y, sum_x * dx, sum_y * dx, sum_yy]
-        for m in range(6):
-            moments[pl.ds(m * TILES + t, 1), :] = jnp.sum(found[m], axis=0, keepdims=True)
-        mixed = jnp.dot(grad_rows, weight, preferred_element_type=F32)
-        for c in range(3):
-            both = mixed[c : c + 1] + mixed[3 + c : 4 + c]
-            moments[pl.ds((6 + c) * TILES + t, 1), :] = both[:, :128] + both[:, 128:]
-        return carry
-
-    lax.fori_loop(0, TILES, back_step, 0)
+    for tile_row in range(2):
+
+        def back_step(k, carry, tile_row=tile_row):
+            tiles = spans(tile_row, k)
+            grad_rows, values = [], []
+            for n, t in enumerate(tiles):
+                pixel_grad = [
+                    two_parts(tile_rows[pl.ds(tile_row * 48 + c * 16 + k * GROUP + n, 1), :])
+                    for c in range(3)
+                ]
+                colour = [two_parts(entry_row(6 + c, t)) for c in range(3)]
+                tops, lows = [g[0] for g in pixel_grad], [g[1] for g in pixel_grad]
+                grad_rows.append(
+                    jnp.concatenate(tops + lows + tops + [jnp.zeros((7, 256), BF16)], axis=0)
+                )
+                colour_rows = jnp.concatenate(
+                    [c[0] for c in colour] * 2
+                    + [c[1] for c in colour]
+                    + [jnp.zeros((7, 128), BF16)],
+                    axis=0,
+                )
+                values.append(
+                    lax.dot_general(
+                        grad_rows[n],
+                        colour_rows,
+                        (((0,), (0,)), ((), ())),
+                        preferred_element_type=F32,
+                    )
+                )
+            gains, laters, mixes = [], [], []
+            for n, t in enumerate(tiles):
+                weight = weights[pixels_of(t), :]
+                mixes.append(jnp.dot(grad_rows[n], weight, preferred_element_type=F32))
+                gain = values[n] * (weight[:, :128].astype(F32) + weight[:, 128:].astype(F32))
+                laters.append(
+                    jnp.dot(
+                        jnp.concatenate(two_parts(gain), axis=1),
+                        tri_after[...],
+                        preferred_element_type=F32,
+                    )
+                )
+                gains.append(gain)
+            for n, t in enumerate(tiles):
+                pull = gains[n] - ratio[pixels_of(t), :] * laters[n]
+                dx = across - entry_row(0, t)
+                center_y = entry_row(1, t)
+                sum_0 = sum_y = sum_yy = None
+                for y in range(16):
+                    dy = (y + 0.5) - center_y
+                    part = pull[16 * y : 16 * y + 16]
+                    part_y = part * dy
+                    part_yy = part_y * dy
+                    sum_0 = part if y == 0 else sum_0 + part
+                    sum_y = part_y if y == 0 else sum_y + part_y
+                    sum_yy = part_yy if y == 0 else sum_yy + part_yy
+                sum_x = sum_0 * dx
+                found = [sum_0, sum_x, sum_y, sum_x * dx, sum_y * dx, sum_yy]
+                for m in range(6):
+                    moments[pl.ds(m * TILES + t, 1), :] = jnp.sum(
+                        found[m], axis=0, keepdims=True
+                    )
+                for c in range(3):
+                    both = mixes[n][c : c + 1] + mixes[n][3 + c : 4 + c]
+                    moments[pl.ds((6 + c) * TILES + t, 1), :] = both[:, :128] + both[:, 128:]
+            return carry
+
+        lax.fori_loop(0, 16 // GROUP, back_step, 0)
 
     feat = [entry[f * TILES : (f + 1) * TILES, :] for f in range(6)]
     mom = [moments[m * TILES : (m + 1) * TILES, :] for m in range(6)]
@@ -657,17 +775,17 @@
 
     acc[...] = jnp.zeros_like(acc)
 
-    def slot_step(b, carry):
-        def pair(ref, at):
-            both = ref[pl.ds(at, 2), :]
-            return jnp.concatenate([both[0:1], both[1:2]], axis=1)
-
-        scatter_block(
-            pair(lists, b * 2), [pair(entry, f * TILES + b * 2) for f in range(FEATS)], acc
+    def slot_step(k, carry):
+        at = [k * 8 + 2 * n for n in range(4)]
+        scatter_blocks(
+            [row_pair(lists, a) for a in at],
+            [[row_pair(entry, f * TILES + a) for f in range(FEATS)] for a in at],
+            hot_list[:, pl.ds(pl.multiple_of(k * 1024, 1024), 1024)],
+            acc,
         )
         return carry
 
-    lax.fori_loop(0, TILES // 2, slot_step, 0)
+    lax.fori_loop(0, TILES // 8, slot_step, 0)
 
     def total_rows(f, h):
         a = acc[pl.ds(pl.multiple_of(f * 32 + h * 8, 8), 8), :]
@@ -686,7 +804,12 @@
         return carry
 
     lax.fori_loop(0, 4, back_pack, 0)
-    send_rows(msg_back, inbox_back, sems.at[8], sems.at[9])
+    each_peer(
+        img,
+        cell,
+        lambda pi, pc: send_message(msg_back, inbox_back, sems.at[8], sems.at[9], pi, pc),
+    )
+    inbox_back[own, :] = msg_back[own, :]
 
     acc[...] = jnp.zeros_like(acc)
     wait_rows(inbox_back, (DEVICES - 1) * PAIRS, sems.at[9])
@@ -703,17 +826,17 @@
 
     lax.fori_loop(0, 8, owner_unpack, 0)
 
-    def owner_step(b, carry):
-        def pair(ref, at):
-            both = ref[pl.ds(at, 2), :]
-            return jnp.concatenate([both[0:1], both[1:2]], axis=1)
-
-        scatter_block(
-            pair(ids_own, b * 2), [pair(table, f * ROWS + b * 2) for f in range(FEATS)], acc
+    def owner_step(k, carry):
+        at = [k * 8 + 2 * n for n in range(4)]
+        scatter_blocks(
+            [row_pair(ids_own, a) for a in at],
+            [[row_pair(table, f * ROWS + a) for f in range(FEATS)] for a in at],
+            hot_own[:, pl.ds(pl.multiple_of(k * 1024, 1024), 1024)],
+            acc,
         )
         return carry
 
-    lax.fori_loop(0, ROWS // 2, owner_step, 0)
+    lax.fori_loop(0, ROWS // 8, owner_step, 0)
 
     def finish(h, carry):
         for f in range(FEATS):
@@ -733,34 +856,48 @@
     wait_rows(msg_back, (DEVICES - 1) * PAIRS, sems.at[8])
 
 
-def pullback_kernel(cam_ref, attr, feat_grad, out, arows):
+def pullback_kernel(cam_ref, attr_hbm, feat_grad, out_hbm, attr, arows, result, load_sems, save_sem):
     cam = read_camera(cam_ref)
-    spread_rows(attr, arows)
+
+    def block(h):
+        return pl.ds(pl.multiple_of(h * 1024, 1024), 1024)
+
+    def load(h):
+        return pltpu.make_async_copy(
+            attr_hbm.at[:, block(h)], attr.at[:, block(h)], load_sems.at[h]
+        )
+
+    for h in range(8):
+        load(h).start()
 
     def step(h, carry):
-        places = attr_rows(h)
+        load(h).wait()
+        for k in range(8):
+            lanes = pl.ds(pl.multiple_of(h * 1024 + k * 128, 128), 128)
+            for g in range(8):
+                n = min(8, ATTRS - 8 * g)
+                arows[g * 64 + 8 * k : g * 64 + 8 * k + n, :] = attr[8 * g : 8 * g + n, lanes]
+        places = [pl.ds((r // 8) * 64 + r % 8, 8, stride=8) for r in range(ATTRS)]
         rows = [arows[at, :] for at in places]
         _, pullback = jax.vjp(lambda r: project(r, cam), rows)
         grads = [
             feat_grad[pl.ds(pl.multiple_of(f * ROWS + h * 8, 8), 8), :] for f in range(FEATS)
         ]
         log_opacity = grads.pop(5)
-        (result,) = pullback(grads)
-        result[10] = log_opacity * (1.0 - jax.nn.sigmoid(rows[10]))
-        for at, v in zip(places, result):
+        (found,) = pullback(grads)
+        found[10] = log_opacity * (1.0 - jax.nn.sigmoid(rows[10]))
+        for at, v in zip(places, found):
             arows[at, :] = v
+        for k in range(8):
+            lanes = pl.ds(pl.multiple_of(h * 1024 + k * 128, 128), 128)
+            for g in range(8):
+                n = min(8, ATTRS - 8 * g)
+                result[8 * g : 8 * g + n, lanes] = arows[g * 64 + 8 * k : g * 64 + 8 * k + n, :]
+        pltpu.make_async_copy(result.at[:, block(h)], out_hbm.at[:, block(h)], save_sem).start()
         return carry
 
     lax.fori_loop(0, 8, step, 0)
-
-    def gather_rows(ct, carry):
-        lanes = pl.ds(pl.multiple_of(ct * 128, 128), 128)
-        for g in range(8):
-            n = min(8, ATTRS - 8 * g)
-            out[8 * g : 8 * g + n, lanes] = arows[pl.ds(pl.multiple_of(g * 512 + ct * 8, 8), n), :]
-        return carry
-
-    lax.fori_loop(0, 64, gather_rows, 0)
+    pltpu.make_async_copy(result, out_hbm, save_sem).wait()
 
 
 def shards(attributes, camera, target, visible_index, tile_lists, tile_len):
@@ -769,11 +906,15 @@
     feat_grad = pl.pallas_call(
         step_kernel,
         out_shape=jax.ShapeDtypeStruct((FEATS * ROWS, 128), F32),
-        in_specs=[smem, smem, vmem, vmem, vmem, vmem],
+        in_specs=[smem, smem, vmem, pl.BlockSpec(memory_space=pl.ANY), vmem, vmem],
         out_specs=vmem,
         scratch_shapes=[
+            pltpu.VMEM((ATTRS, 8192), F32),
             pltpu.VMEM((4096, 128), F32),
             pltpu.VMEM((FEATS * ROWS, 128), F32),
+            pltpu.VMEM((FEATS * 32, 768), BF16),
+            pltpu.VMEM((256, TILES * LIST), BF16),
+            pltpu.VMEM((256, ROWS * 128), BF16),
             pltpu.VMEM((DEVICES, 128), I32),
             pltpu.VMEM((ROWS, 128), I32),
             pltpu.VMEM((DEVICES * 8, 128), F32),
@@ -793,7 +934,7 @@
             pltpu.VMEM((3 * 3 * 3 * 48, 128), F32),
             pltpu.VMEM((2 * 3 * 48, 384), F32),
             pltpu.VMEM((2 * FEATS * 32, 256), F32),
-            pltpu.SemaphoreType.DMA((10,)),
+            pltpu.SemaphoreType.DMA((11,)),
         ],
         compiler_params=pltpu.CompilerParams(
             collective_id=0, has_side_effects=True, vmem_limit_bytes=56 * 1024 * 1024
@@ -810,9 +951,15 @@
     return pl.pallas_call(
         pullback_kernel,
         out_shape=jax.ShapeDtypeStruct(attributes.shape, F32),
-        in_specs=[smem, vmem, vmem],
-        out_specs=vmem,
-        scratch_shapes=[pltpu.VMEM((4096, 128), F32)],
+        in_specs=[smem, pl.BlockSpec(memory_space=pl.ANY), vmem],
+        out_specs=pl.BlockSpec(memory_space=pl.ANY),
+        scratch_shapes=[
+            pltpu.VMEM((ATTRS, 8192), F32),
+            pltpu.VMEM((512, 128), F32),
+            pltpu.VMEM((ATTRS, 8192), F32),
+            pltpu.SemaphoreType.DMA((8,)),
+            pltpu.SemaphoreType.DMA,
+        ],
         name="splat_pullback",
     )(camera, attributes, feat_grad)
 

time: 103 us -> 77.1 us (0.75)
  Pallas kernels: 103 us -> 76.9 us
    pallas_call x1, Pallas kernels: 97.2 us -> 72.3 us  [shards(): pl.pallas_call(step_kernel, out_shape=jax.ShapeDtypeStruct((FEATS * ROWS,...]
where the time goes in v2:
time: 77.1 us; the launch traced here: 76.9 us
  Pallas kernels  76.9 us (100%)
    pallas_call x1, Pallas kernels, shards(): pl.pallas_call(step_kernel, out_shape=jax.ShapeDtypeStruct((FEATS * ROWS,...  72.3 us
    pallas_call x1, Pallas kernels, shards(): pl.pallas_call(pullback_kernel, out_shape=jax.ShapeDtypeStruct(attributes...  4.55 us

profile of v2, /device:TPU:1, one launch (start us, length us, event | category | flops | bytes accessed | tf_op | source)
XLA Modules:
  0.0 76.9 jit_solution(935927725422382130)
XLA Ops:
  0.0 72.3 %splat_step.1.feat_grad = f32[576,128]{1,0:T(8,128)} custom-call(f32[3,3]{1,0:T(4,128)} %cam_ref.3, s32[2,16]{1,0:T(2,128)} %len_ref.1, s32[64,128]{1,0:T(8,128)} %bitcast.2, f32[59,8192]{1,0:T(8,128)} %attr_hbm.3, f32[3,32,256]{2,1,0:T(8,128)} %target.1, s32[32,128]{1,0:T(8,128)} %bitcast.3), custom_call_target="tpu_custom_call" | custom-call | tf_op jit(solution)/shard_map/splat_step/pallas_call | solution.py:906
  72.3 4.6 %splat_pullback.1 = f32[59,8192]{1,0:T(8,128)} custom-call(f32[3,3]{1,0:T(4,128)} %cam_ref.3, f32[59,8192]{1,0:T(8,128)} %attr_hbm.3, f32[576,128]{1,0:T(8,128)} %splat_step.1.feat_grad), custom_call_target="tpu_custom_call" | custom-call | tf_op jit(solution)/shard_map/splat_pullback/pallas_call | solution.py:951

commit v3 on v2

--- a/solution.py
+++ b/solution.py
@@ -22,6 +22,8 @@
 ROWS = 64
 FEATS = 9
 PAIRS = 5
+EXACT = 5
+BLOCKS = 8
 GROUP = 4
 
 WEIGHT_SSIM = 0.2
@@ -143,14 +145,19 @@
 
 
 def each_peer(img, cell, act):
-    for i in range(N_IMG):
+    base = wrap(cell + 8, N_CELL)
+    for i in (4, 5, 3, 2, 6, 1, 7, 0):
         pi = wrap(img + i, N_IMG) if i else img
 
         def step(j, carry, pi=pi):
-            act(pi, wrap(cell + j, N_CELL))
+            act(pi, wrap(base + j, N_CELL))
             return carry
 
-        lax.fori_loop(0 if i else 1, N_CELL, step, 0)
+        if i:
+            lax.fori_loop(0, N_CELL, step, 0)
+        else:
+            lax.fori_loop(0, 8, step, 0)
+            lax.fori_loop(9, N_CELL, step, 0)
 
 
 def left_half():
@@ -191,36 +198,40 @@
     return jnp.concatenate([both[0:1], both[1:2]], axis=1)
 
 
-def make_parts(table, parts):
+def make_parts(table, parts, thirds):
     for f in range(FEATS):
+        rows = slice(32 * f, 32 * f + 32)
         for half in range(2):
             v = table[pl.ds(f * ROWS + half, 32, stride=2), :]
-            for part in range(3):
-                top = v.astype(BF16)
-                parts[
-                    32 * f : 32 * f + 32, 256 * part + 128 * half : 256 * part + 128 * half + 128
-                ] = top
-                v = v - top.astype(F32)
-
-
-def gather_blocks(parts, ids, hots):
-    found = [
-        jnp.dot(
-            parts[...], jnp.concatenate([hot] * 3, axis=0), preferred_element_type=F32
+            top = v.astype(BF16)
+            v = v - top.astype(F32)
+            middle = v.astype(BF16)
+            parts[rows, 128 * half : 128 * half + 128] = top
+            parts[rows, 256 + 128 * half : 384 + 128 * half] = middle
+            if f < EXACT:
+                low = (v - middle.astype(F32)).astype(BF16)
+                thirds[rows, 128 * half : 128 * half + 128] = low
+
+
+def gather_blocks(parts, thirds, ids, hots):
+    found, fine = [], []
+    for hot in hots:
+        found.append(
+            jnp.dot(
+                parts[...], jnp.concatenate([hot] * 2, axis=0), preferred_element_type=F32
+            )
         )
-        for hot in hots
-    ]
+        fine.append(jnp.dot(thirds[...], hot, preferred_element_type=F32))
     out = []
-    for v, block in zip(found, ids):
+    for v, low, block in zip(found, fine, ids):
         mask = lax.broadcasted_iota(I32, (32, 256), 0) == split_ids(block)[0]
-        out.append(
-            [
-                jnp.sum(
-                    jnp.where(mask, v[32 * f : 32 * f + 32], 0.0), axis=0, keepdims=True
-                )
-                for f in range(FEATS)
-            ]
-        )
+        rows = []
+        for f in range(FEATS):
+            value = v[32 * f : 32 * f + 32]
+            if f < EXACT:
+                value = value + low[32 * f : 32 * f + 32]
+            rows.append(jnp.sum(jnp.where(mask, value, 0.0), axis=0, keepdims=True))
+        out.append(rows)
     return out
 
 
@@ -260,24 +271,40 @@
     return z
 
 
-def border_block(lane_tile, row_block):
-    return (lane_tile * 4 + row_block) * 48
+NORTH, SOUTH, PACK_WEST, PACK_EAST, FROM_WEST, FROM_EAST = 192, 288, 384, 400, 416, 432
+FROM_NW, FROM_NE, FROM_SW, FROM_SE, EXT_ROWS = 448, 456, 464, 472, 480
+BORDER_ROWS = 256
+
+
+def pack_columns(ext):
+    lane = lax.broadcasted_iota(I32, (8, 128), 1)
+    for t in range(2):
+        west = jnp.zeros((8, 128), F32)
+        east = west
+        for k in range(6):
+            here = (lane >= 16 * k) & (lane < 16 * k + 16)
+            at = t * 48 + 8 * k
+            first, last = ext[at : at + 8, :], ext[96 + at : 104 + at, :]
+            west = jnp.where(here, pltpu.roll(first, 16 * k, 1) if k else first, west)
+            east = jnp.where(here, pltpu.roll(last, 16 * k + 16, 1), east)
+        ext[PACK_WEST + 8 * t : PACK_WEST + 8 * t + 8, :] = west
+        ext[PACK_EAST + 8 * t : PACK_EAST + 8 * t + 8, :] = east
 
 
 def border_copies(ext, img, cell, send, recv):
     west, east = jnp.where(cell == 0, N_CELL - 1, cell - 1), wrap(cell + 1, N_CELL)
     north, south = jnp.where(img == 0, N_IMG - 1, img - 1), wrap(img + 1, N_IMG)
     plan = [
-        (border_block(1, 1), border_block(3, 1), 96, img, west),
-        (border_block(2, 1), border_block(0, 1), 96, img, east),
+        (PACK_WEST, FROM_SE, 8, north, west),
+        (PACK_EAST, FROM_SW, 8, north, east),
+        (PACK_WEST + 8, FROM_NE, 8, south, west),
+        (PACK_EAST + 8, FROM_NW, 8, south, east),
+        (PACK_WEST, FROM_EAST, 16, img, west),
+        (PACK_EAST, FROM_WEST, 16, img, east),
     ]
-    for lane_tile in (1, 2):
-        plan.append((border_block(lane_tile, 1), border_block(lane_tile, 3), 48, north, cell))
-        plan.append((border_block(lane_tile, 2), border_block(lane_tile, 0), 48, south, cell))
-    plan.append((border_block(1, 1), border_block(3, 3), 48, north, west))
-    plan.append((border_block(2, 1), border_block(0, 3), 48, north, east))
-    plan.append((border_block(1, 2), border_block(3, 0), 48, south, west))
-    plan.append((border_block(2, 2), border_block(0, 0), 48, south, east))
+    for k in range(2):
+        plan.append((96 * k, SOUTH + 48 * k, 48, north, cell))
+        plan.append((96 * k + 48, NORTH + 48 * k, 48, south, cell))
     for source, dest, count, to_img, to_cell in plan:
         pltpu.make_async_remote_copy(
             src_ref=ext.at[pl.ds(source, count)],
@@ -289,49 +316,50 @@
         ).start()
 
 
-BORDER_ROWS = 2 * 96 + 8 * 48
-
-
 def wait_rows(ref, count, sem):
     part = ref.at[pl.ds(0, count)]
     pltpu.make_async_copy(part, part, sem).wait()
 
 
-def window(ext, img, cell, c, row_block):
-    left = lax.broadcasted_iota(I32, (16, 128), 1) < 64
-    tiles = []
-    for lane_tile in range(4):
-        v = ext[pl.ds(border_block(lane_tile, row_block) + c * 16, 16), :]
-        bad = None
-        if lane_tile == 0:
-            bad = cell == 0
-        if lane_tile == 3:
-            bad = cell == N_CELL - 1
-        if row_block == 0:
-            bad = (img == 0) if bad is None else jnp.logical_or(bad, img == 0)
-        if row_block == 3:
-            bad = (img == N_IMG - 1) if bad is None else jnp.logical_or(bad, img == N_IMG - 1)
-        if bad is not None:
-            v = v * jnp.where(bad, 0.0, 1.0)
-        tiles.append(pltpu.roll(v, 64, 1))
-    return [jnp.where(left, tiles[j], tiles[j + 1]) for j in range(3)]
-
-
-def blur_down(ref, base, first, count):
-    out = []
+def window(ext, img, cell, c, row_block, half):
+    lane = lax.broadcasted_iota(I32, (8, 128), 1)
+    at = 16 * c + 8 * half
+    bases = [NORTH, 0, 48, SOUTH][row_block]
+    step = 48 if row_block in (0, 3) else 96
+    sides = [
+        (FROM_NW, FROM_NE),
+        (FROM_WEST, FROM_EAST),
+        (FROM_WEST + 8, FROM_EAST + 8),
+        (FROM_SW, FROM_SE),
+    ][row_block]
+    first = pltpu.roll(ext[bases + at : bases + at + 8, :], 64, 1)
+    second = pltpu.roll(ext[bases + step + at : bases + step + at + 8, :], 64, 1)
+    block = 16 * (2 * c + half)
+    left = pltpu.roll(ext[sides[0] : sides[0] + 8, :], (48 - block) % 128, 1)
+    right = pltpu.roll(ext[sides[1] : sides[1] + 8, :], (64 - block) % 128, 1)
+    keep_left = jnp.where(cell == 0, 64, 48)
+    keep_right = jnp.where(cell == N_CELL - 1, 64, 80)
+    tiles = [
+        jnp.where(lane < 64, jnp.where(lane >= keep_left, left, 0.0), first),
+        jnp.where(lane < 64, first, second),
+        jnp.where(lane < 64, second, jnp.where(lane < keep_right, right, 0.0)),
+    ]
+    if row_block == 0:
+        tiles = [v * jnp.where(img == 0, 0.0, 1.0) for v in tiles]
+    if row_block == 3:
+        tiles = [v * jnp.where(img == N_IMG - 1, 0.0, 1.0) for v in tiles]
+    return tiles
+
+
+def blur(ref, start, stride):
+    down = []
     for j in range(3):
-        start, stride = base
-        at = start + j * stride + first
-        total = TAPS[5] * ref[pl.ds(at + 5, count), :]
+        at = start + j * stride
+        total = TAPS[5] * ref[pl.ds(at + 5, 8), :]
         for o in range(5):
-            total = total + TAPS[o] * (
-                ref[pl.ds(at + o, count), :] + ref[pl.ds(at + 10 - o, count), :]
-            )
-        out.append(total)
-    return jnp.concatenate(out, axis=1)
-
-
-def blur_along(v):
+            total = total + TAPS[o] * (ref[pl.ds(at + o, 8), :] + ref[pl.ds(at + 10 - o, 8), :])
+        down.append(total)
+    v = jnp.concatenate(down, axis=1)
     total = TAPS[5] * v
     for o in range(5):
         d = 5 - o
@@ -350,8 +378,8 @@
     return upper / lower
 
 
-def map_base(m, c):
-    return ((m * 3 + c) * 3 * 64, 64)
+def map_row(m, c):
+    return (m * 3 + c) * 3 * 64
 
 
 def step_kernel(
@@ -366,6 +394,7 @@
     arows,
     table,
     parts,
+    thirds,
     hot_list,
     hot_own,
     ids_in,
@@ -404,12 +433,14 @@
     load_attr = pltpu.make_async_copy(attr_hbm, attr, sems.at[10])
     load_attr.start()
 
-    for lane_tile in range(2):
+    for k in range(2):
         for t in range(2):
             for c in range(3):
-                ext_target[pl.ds(border_block(1 + lane_tile, 1 + t) + c * 16, 16), :] = target[
-                    c, 16 * t : 16 * t + 16, 128 * lane_tile : 128 * lane_tile + 128
+                at = 96 * k + 48 * t + 16 * c
+                ext_target[at : at + 16, :] = target[
+                    c, 16 * t : 16 * t + 16, 128 * k : 128 * k + 128
                 ]
+    pack_columns(ext_target)
 
     def list_hot(b, carry):
         hot_list[:, pl.ds(pl.multiple_of(b * 256, 256), 256)] = one_hot(
@@ -432,7 +463,7 @@
         return carry
 
     lax.fori_loop(0, 8, project_step, 0)
-    make_parts(table, parts)
+    make_parts(table, parts, thirds)
 
     row_at = lax.broadcasted_iota(I32, (128, 128), 0)
     lane_at = lax.broadcasted_iota(I32, (128, 128), 1)
@@ -462,16 +493,21 @@
     wait_rows(ext_target, BORDER_ROWS, sems.at[3])
     for c in range(3):
         for row_block in range(4):
-            strips = window(ext_target, img, cell, c, row_block)
-            for j in range(3):
-                for m, v in ((3, strips[j]), (4, strips[j] * strips[j])):
-                    start, stride = map_base(m, c)
-                    maps[pl.ds(start + j * stride + row_block * 16, 16), :] = v
-    for m in (3, 4):
-        for c in range(3):
-            blurred[pl.ds(((m - 3) * 3 + c) * 48, 48), :] = blur_along(
-                blur_down(maps, map_base(m, c), 6, 48)
-            )
+            for half in range(2):
+                strips = window(ext_target, img, cell, c, row_block, half)
+                for j in range(3):
+                    for m, v in ((3, strips[j]), (4, strips[j] * strips[j])):
+                        at = map_row(m, c) + 64 * j + 16 * row_block + 8 * half
+                        maps[at : at + 8, :] = v
+
+    def target_blur(c, carry):
+        for m in range(2):
+            for r in range(6):
+                at = pl.multiple_of((m * 3 + c) * 48 + 8 * r, 8)
+                blurred[pl.ds(at, 8), :] = blur(maps, map_row(3 + m, c) + 6 + 8 * r, 64)
+        return carry
+
+    lax.fori_loop(0, 3, target_blur, 0)
 
     wait_rows(ids_in, DEVICES - 1, sems.at[1])
     odd = me - (me // 2) * 2
@@ -503,7 +539,7 @@
         hots = [one_hot(split_ids(v)[1]) for v in ids]
         for n in range(4):
             hot_own[:, pl.ds(pl.multiple_of(g * 1024 + n * 256, 256), 256)] = hots[n]
-        got = gather_blocks(parts, ids, hots)
+        got = gather_blocks(parts, thirds, ids, hots)
         for n in range(4):
             for row in range(2):
                 d = g * 8 + 2 * n + row
@@ -548,11 +584,12 @@
         return carry
 
     lax.fori_loop(0, 8, table_step, 0)
-    make_parts(table, parts)
+    make_parts(table, parts, thirds)
 
     def list_step(k, carry):
         got = gather_blocks(
             parts,
+            thirds,
             [row_pair(lists, k * 8 + 2 * n) for n in range(4)],
             [
                 hot_list[:, pl.ds(pl.multiple_of(k * 1024 + n * 256, 256), 256)]
@@ -636,63 +673,85 @@
         lax.fori_loop(0, 16 // GROUP, render_step, 0)
 
     picture = swap_blocks(tile_rows[...])
-    for lane_tile in range(2):
-        ext_render[pl.ds(border_block(1 + lane_tile, 1), 96), :] = picture[
-            :, 128 * lane_tile : 128 * lane_tile + 128
-        ]
+    for k in range(2):
+        ext_render[96 * k : 96 * k + 96, :] = picture[:, 128 * k : 128 * k + 128]
+    pack_columns(ext_render)
     border_copies(ext_render, img, cell, sems.at[6], sems.at[7])
     wait_rows(ext_render, BORDER_ROWS, sems.at[7])
 
     for c in range(3):
         for row_block in range(4):
-            parts = window(ext_render, img, cell, c, row_block)
-            start, stride = map_base(3, c)
+            for half in range(2):
+                strips = window(ext_render, img, cell, c, row_block, half)
+                for j in range(3):
+                    at = 64 * j + 16 * row_block + 8 * half
+                    v = strips[j]
+                    wanted = maps[map_row(3, c) + at : map_row(3, c) + at + 8, :]
+                    for m, value in ((0, v), (1, v * v), (2, v * wanted)):
+                        maps[map_row(m, c) + at : map_row(m, c) + at + 8, :] = value
+    row_at = lax.broadcasted_iota(I32, (8, 384), 0) + (img * 32 - 5)
+    lane_at = lax.broadcasted_iota(I32, (8, 384), 1) + (cell * 256 - 64)
+    inside = (lane_at >= 0) & (lane_at < N_CELL * 256)
+
+    def similarity_step(c, carry):
+        for r in range(6):
+            mean, square, cross = [blur(maps, map_row(m, c) + 6 + 8 * r, 64) for m in range(3)]
+            mean_target, square_target = [
+                blurred[pl.ds(pl.multiple_of((m * 3 + c) * 48 + 8 * r, 8), 8), :]
+                for m in range(2)
+            ]
+            _, pullback = jax.vjp(
+                lambda x, y, z, mt=mean_target, st=square_target: ssim_value(x, mt, y, st, z),
+                mean,
+                square,
+                cross,
+            )
+            keep = inside & (row_at + 8 * r >= 0) & (row_at + 8 * r < N_IMG * 32)
+            for m, v in enumerate(pullback(jnp.full((8, 384), -WEIGHT_SSIM, F32))):
+                v = jnp.where(keep, v, 0.0)
+                for j in range(3):
+                    at = pl.multiple_of(((m * 3 + c) * 3 + j) * 48 + 8 * r, 8)
+                    coefs[pl.ds(at, 8), :] = v[:, 128 * j : 128 * j + 128]
+        return carry
+
+    lax.fori_loop(0, 3, similarity_step, 0)
+    left = left_half()
+
+    def image_step(c, carry):
+        for r in range(4):
+            back_mean, back_square, back_cross = [
+                blur(coefs, (m * 3 + c) * 3 * 48 + 8 * r, 48) for m in range(3)
+            ]
+            found = []
             for j in range(3):
-                rows = pl.ds(start + j * stride + row_block * 16, 16)
-                v = parts[j]
-                for m, value in ((0, v), (1, v * v), (2, v * maps[rows, :])):
-                    first, step = map_base(m, c)
-                    maps[pl.ds(first + j * step + row_block * 16, 16), :] = value
-    row_at = lax.broadcasted_iota(I32, (48, 384), 0) + (img * 32 - 5)
-    lane_at = lax.broadcasted_iota(I32, (48, 384), 1) + (cell * 256 - 64)
-    inside = (row_at >= 0) & (row_at < N_IMG * 32) & (lane_at >= 0) & (lane_at < N_CELL * 256)
-    for c in range(3):
-        mean, square, cross = [
-            blur_along(blur_down(maps, map_base(m, c), 6, 48)) for m in range(3)
-        ]
-        mean_target = blurred[pl.ds(c * 48, 48), :]
-        square_target = blurred[pl.ds((3 + c) * 48, 48), :]
-        similarity, pullback = jax.vjp(
-            lambda a, b, d: ssim_value(a, mean_target, b, square_target, d), mean, square, cross
-        )
-        for m, v in enumerate(pullback(jnp.full((48, 384), -WEIGHT_SSIM, F32))):
-            v = jnp.where(inside, v, 0.0)
-            for j in range(3):
-                coefs[pl.ds(((m * 3 + c) * 3 + j) * 48, 48), :] = v[:, 128 * j : 128 * j + 128]
-    for c in range(3):
-        back_mean, back_square, back_cross = [
-            blur_along(blur_down(coefs, ((m * 3 + c) * 3 * 48, 48), 0, 32))[:, 64:320]
-            for m in range(3)
-        ]
-        for t in range(2):
-            rows = slice(16 * t, 16 * t + 16)
-            image = jnp.concatenate(
-                [
-                    ext_render[pl.ds(border_block(1 + k, 1 + t) + c * 16, 16), :]
-                    for k in range(2)
-                ],
+                lanes = slice(128 * j, 128 * j + 128)
+                at = 64 * j + 16 + 8 * r
+                image = maps[pl.ds(pl.multiple_of(map_row(0, c) + at, 8), 8), :]
+                wanted = maps[pl.ds(pl.multiple_of(map_row(3, c) + at, 8), 8), :]
+                difference = image - wanted
+                slope = (
+                    (1.0 - WEIGHT_SSIM)
+                    * difference
+                    / jnp.sqrt(difference * difference + SMOOTHING * SMOOTHING)
+                )
+                found.append(
+                    pltpu.roll(
+                        slope
+                        + back_mean[:, lanes]
+                        + 2.0 * image * back_square[:, lanes]
+                        + wanted * back_cross[:, lanes],
+                        64,
+                        1,
+                    )
+                )
+            at = pl.multiple_of((r // 2) * 48 + c * 16 + (r % 2) * 8, 8)
+            tile_rows[pl.ds(at, 8), :] = jnp.concatenate(
+                [jnp.where(left, found[0], found[1]), jnp.where(left, found[1], found[2])],
                 axis=1,
             )
-            wanted = target[c, rows, :]
-            difference = image - wanted
-            tile_rows[pl.ds(t * 48 + c * 16, 16), :] = (
-                (1.0 - WEIGHT_SSIM)
-                * difference
-                / jnp.sqrt(difference * difference + SMOOTHING * SMOOTHING)
-                + back_mean[rows]
-                + 2.0 * image * back_square[rows]
-                + wanted * back_cross[rows]
-            )
+        return carry
+
+    lax.fori_loop(0, 3, image_step, 0)
     tile_rows[...] = swap_blocks(tile_rows[...])
 
     for tile_row in range(2):
@@ -776,16 +835,16 @@
     acc[...] = jnp.zeros_like(acc)
 
     def slot_step(k, carry):
-        at = [k * 8 + 2 * n for n in range(4)]
+        at = [k * 2 * BLOCKS + 2 * n for n in range(BLOCKS)]
         scatter_blocks(
             [row_pair(lists, a) for a in at],
             [[row_pair(entry, f * TILES + a) for f in range(FEATS)] for a in at],
-            hot_list[:, pl.ds(pl.multiple_of(k * 1024, 1024), 1024)],
+            hot_list[:, pl.ds(pl.multiple_of(k * 256 * BLOCKS, 256), 256 * BLOCKS)],
             acc,
         )
         return carry
 
-    lax.fori_loop(0, TILES // 8, slot_step, 0)
+    lax.fori_loop(0, TILES // (2 * BLOCKS), slot_step, 0)
 
     def total_rows(f, h):
         a = acc[pl.ds(pl.multiple_of(f * 32 + h * 8, 8), 8), :]
@@ -827,16 +886,16 @@
     lax.fori_loop(0, 8, owner_unpack, 0)
 
     def owner_step(k, carry):
-        at = [k * 8 + 2 * n for n in range(4)]
+        at = [k * 2 * BLOCKS + 2 * n for n in range(BLOCKS)]
         scatter_blocks(
             [row_pair(ids_own, a) for a in at],
             [[row_pair(table, f * ROWS + a) for f in range(FEATS)] for a in at],
-            hot_own[:, pl.ds(pl.multiple_of(k * 1024, 1024), 1024)],
+            hot_own[:, pl.ds(pl.multiple_of(k * 256 * BLOCKS, 256), 256 * BLOCKS)],
             acc,
         )
         return carry
 
-    lax.fori_loop(0, ROWS // 8, owner_step, 0)
+    lax.fori_loop(0, ROWS // (2 * BLOCKS), owner_step, 0)
 
     def finish(h, carry):
         for f in range(FEATS):
@@ -912,7 +971,8 @@
             pltpu.VMEM((ATTRS, 8192), F32),
             pltpu.VMEM((4096, 128), F32),
             pltpu.VMEM((FEATS * ROWS, 128), F32),
-            pltpu.VMEM((FEATS * 32, 768), BF16),
+            pltpu.VMEM((FEATS * 32, 512), BF16),
+            pltpu.VMEM((EXACT * 32, 256), BF16),
             pltpu.VMEM((256, TILES * LIST), BF16),
             pltpu.VMEM((256, ROWS * 128), BF16),
             pltpu.VMEM((DEVICES, 128), I32),
@@ -921,8 +981,8 @@
             pltpu.VMEM((DEVICES * 8, 128), F32),
             pltpu.VMEM((DEVICES * 8, 128), F32),
             pltpu.VMEM((DEVICES * 8, 128), F32),
-            pltpu.VMEM((16 * 48, 128), F32),
-            pltpu.VMEM((16 * 48, 128), F32),
+            pltpu.VMEM((EXT_ROWS, 128), F32),
+            pltpu.VMEM((EXT_ROWS, 128), F32),
             pltpu.VMEM((FEATS * TILES, 128), F32),
             pltpu.VMEM((256, 128), BF16),
             pltpu.VMEM((256, 128), BF16),

time: 77.1 us -> 73 us (0.947)
  Pallas kernels: 76.9 us -> 72.8 us
    pallas_call x1, Pallas kernels: 72.3 us -> 68.2 us  [shards(): pl.pallas_call(step_kernel, out_shape=jax.ShapeDtypeStruct((FEATS * ROWS,...]
where the time goes in v3:
time: 73 us; the launch traced here: 72.8 us
  Pallas kernels  72.8 us (100%)
    pallas_call x1, Pallas kernels, shards(): pl.pallas_call(step_kernel, out_shape=jax.ShapeDtypeStruct((FEATS * ROWS,...  68.2 us
    pallas_call x1, Pallas kernels, shards(): pl.pallas_call(pullback_kernel, out_shape=jax.ShapeDtypeStruct(attributes...  4.55 us

profile of v3, /device:TPU:1, one launch (start us, length us, event | category | flops | bytes accessed | tf_op | source)
XLA Modules:
  0.0 72.8 jit_solution(6269856412556008174)
XLA Ops:
  0.0 68.2 %splat_step.1.feat_grad = f32[576,128]{1,0:T(8,128)} custom-call(f32[3,3]{1,0:T(4,128)} %cam_ref.3, s32[2,16]{1,0:T(2,128)} %len_ref.1, s32[64,128]{1,0:T(8,128)} %bitcast.2, f32[59,8192]{1,0:T(8,128)} %attr_hbm.3, f32[3,32,256]{2,1,0:T(8,128)} %target.1, s32[32,128]{1,0:T(8,128)} %bitcast.3), custom_call_target="tpu_custom_call" | custom-call | tf_op jit(solution)/shard_map/splat_step/pallas_call | solution.py:965
  68.2 4.6 %splat_pullback.1 = f32[59,8192]{1,0:T(8,128)} custom-call(f32[3,3]{1,0:T(4,128)} %cam_ref.3, f32[59,8192]{1,0:T(8,128)} %attr_hbm.3, f32[576,128]{1,0:T(8,128)} %splat_step.1.feat_grad), custom_call_target="tpu_custom_call" | custom-call | tf_op jit(solution)/shard_map/splat_pullback/pallas_call | solution.py:1011

commit v4 on v3

--- a/solution.py
+++ b/solution.py
@@ -144,20 +144,50 @@
     return jnp.where(value >= count, value - count, value)
 
 
-def each_peer(img, cell, act):
-    base = wrap(cell + 8, N_CELL)
-    for i in (4, 5, 3, 2, 6, 1, 7, 0):
-        pi = wrap(img + i, N_IMG) if i else img
-
-        def step(j, carry, pi=pi):
-            act(pi, wrap(base + j, N_CELL))
-            return carry
-
-        if i:
-            lax.fori_loop(0, N_CELL, step, 0)
-        else:
-            lax.fori_loop(0, 8, step, 0)
-            lax.fori_loop(9, N_CELL, step, 0)
+def ring_distance(d):
+    return min(d, 4 - d)
+
+
+STEPS = sorted(
+    ((dy, dz) for dy in range(4) for dz in range(4)),
+    key=lambda s: ring_distance(s[0]) + ring_distance(s[1]),
+)
+
+
+def pick(index, values):
+    found = values[0]
+    for n in range(1, len(values)):
+        found = jnp.where(index == n, values[n], found)
+    return found
+
+
+class Place:
+    def __init__(self, img, cell):
+        self.y, self.z = lax.div(img, 2), lax.div(cell, 4)
+        core, x = img - self.y * 2, cell - self.z * 4
+        self.cores = [core, 1 - core]
+        self.xs = [wrap(x + dx, 4) if dx else x for dx in range(4)]
+        self.x_halves = [lax.div(v, 2) for v in self.xs]
+
+    def devices(self, dy, dz):
+        row, column = wrap(self.y + dy, 4) * 2, wrap(self.z + dz, 4)
+        found = []
+        for q in range(8):
+            pi = row + self.cores[q % 2]
+            found.append((pi, column * 4 + self.xs[q // 2], pi * 8 + column * 2 + self.x_halves[q // 2]))
+        return found
+
+
+def opposite(q):
+    return (4 - q // 2) % 4 * 2 + q % 2
+
+
+def each_step(place, act):
+    for dy, dz in reversed(STEPS):
+        seen = STEPS.index(((4 - dy) % 4, (4 - dz) % 4))
+        for q, (pi, pc, half) in enumerate(place.devices(dy, dz)):
+            if (dy, dz, q) != (0, 0, 0):
+                act(pi, pc, half, seen * 8 + opposite(q), seen // 2)
 
 
 def left_half():
@@ -417,16 +447,18 @@
     blurred,
     acc,
     sems,
+    id_sems,
+    back_sems,
 ):
     img = lax.axis_index("img")
     cell = lax.axis_index("cell")
     me = img * N_CELL + cell
 
     barrier = pltpu.get_barrier_semaphore()
-    each_peer(
-        img,
-        cell,
-        lambda pi, pc: pl.semaphore_signal(
+    place = Place(img, cell)
+    each_step(
+        place,
+        lambda pi, pc, *_: pl.semaphore_signal(
             barrier, 1, device_id=(pi, pc), device_id_type=MESH
         ),
     )
@@ -475,20 +507,21 @@
 
     pl.semaphore_wait(barrier, DEVICES - 1)
 
-    def send_ids(pi, pc):
-        p = pi * N_CELL + pc
+    def send_ids(pi, pc, half, rank, group):
         pltpu.make_async_remote_copy(
-            src_ref=vis.at[pl.ds(p // 2, 1)],
-            dst_ref=ids_in.at[pl.ds(me, 1)],
+            src_ref=vis.at[pl.ds(half, 1)],
+            dst_ref=ids_in.at[pl.ds(rank, 1)],
             send_sem=sems.at[0],
-            recv_sem=sems.at[1],
+            recv_sem=id_sems.at[group],
             device_id=(pi, pc),
             device_id_type=MESH,
         ).start()
 
-    each_peer(img, cell, send_ids)
+    each_step(place, send_ids)
+    pltpu.make_async_copy(
+        vis.at[pl.ds(me // 2, 1)], ids_in.at[pl.ds(0, 1)], id_sems.at[0]
+    ).start()
     border_copies(ext_target, img, cell, sems.at[2], sems.at[3])
-    ids_in[pl.ds(me, 1), :] = vis[pl.ds(me // 2, 1), :]
 
     wait_rows(ext_target, BORDER_ROWS, sems.at[3])
     for c in range(3):
@@ -509,67 +542,58 @@
 
     lax.fori_loop(0, 3, target_blur, 0)
 
-    wait_rows(ids_in, DEVICES - 1, sems.at[1])
     odd = me - (me // 2) * 2
     left = left_half()
-    for c in range(8):
-        first = ids_in[8 * c : 8 * c + 8, :]
-        second = ids_in[64 + 8 * c : 72 + 8 * c, :]
+    left_row = lax.broadcasted_iota(I32, (1, 128), 1) < 64
+
+    def reply_step(g, carry):
+        wait_rows(ids_in, 16, id_sems.at[g])
+        at = pl.multiple_of(g * 16, 8)
+        first, second = ids_in[pl.ds(at, 8), :], ids_in[pl.ds(at + 8, 8), :]
         even_form = jnp.where(left, first, pltpu.roll(second, 64, 1))
         odd_form = jnp.where(left, pltpu.roll(first, 64, 1), second)
-        ids_own[8 * c : 8 * c + 8, :] = jnp.where(odd == 0, even_form, odd_form)
-
-    def send_message(source, dest, send, recv, pi, pc):
-        pltpu.make_async_remote_copy(
-            src_ref=source.at[pl.ds(pl.multiple_of((pi * N_CELL + pc) * 8, 8), PAIRS)],
-            dst_ref=dest.at[pl.ds(pl.multiple_of(me * 8, 8), PAIRS)],
-            send_sem=send,
-            recv_sem=recv,
-            device_id=(pi, pc),
-            device_id_type=MESH,
-        ).start()
-
-    left_row = lax.broadcasted_iota(I32, (1, 128), 1) < 64
-    half_img = img - (img // 4) * 4
-    own_group = half_img * 2 + cell // 8
-
-    def reply_step(k, carry):
-        g = wrap(own_group + 1 + k, 8)
-        ids = [row_pair(ids_own, g * 8 + 2 * n) for n in range(4)]
+        both = jnp.where(odd == 0, even_form, odd_form)
+        ids_own[pl.ds(pl.multiple_of(g * 8, 8), 8), :] = both
+        ids = [
+            jnp.concatenate([both[2 * n : 2 * n + 1], both[2 * n + 1 : 2 * n + 2]], axis=1)
+            for n in range(4)
+        ]
         hots = [one_hot(split_ids(v)[1]) for v in ids]
         for n in range(4):
             hot_own[:, pl.ds(pl.multiple_of(g * 1024 + n * 256, 256), 256)] = hots[n]
         got = gather_blocks(parts, thirds, ids, hots)
         for n in range(4):
             for row in range(2):
-                d = g * 8 + 2 * n + row
+                d = g * 128 + (2 * n + row) * 8
                 for i in range(PAIRS):
-                    first = got[n][2 * i][:, 128 * row : 128 * row + 128]
-                    second = got[n][min(2 * i + 1, FEATS - 1)][:, 128 * row : 128 * row + 128]
-                    msg[pl.ds(d * 8 + i, 1), :] = jnp.where(
-                        left_row, first, pltpu.roll(second, 64, 1)
-                    )
-                    msg[pl.ds(512 + d * 8 + i, 1), :] = jnp.where(
-                        left_row, pltpu.roll(first, 64, 1), second
+                    low = got[n][2 * i][:, 128 * row : 128 * row + 128]
+                    high = got[n][min(2 * i + 1, FEATS - 1)][:, 128 * row : 128 * row + 128]
+                    msg[pl.ds(d + i, 1), :] = jnp.where(left_row, low, pltpu.roll(high, 64, 1))
+                    msg[pl.ds(d + 64 + i, 1), :] = jnp.where(
+                        left_row, pltpu.roll(low, 64, 1), high
                     )
         for side in range(2):
-            to_img = 4 * side + g // 2
-
-            def send_step(n, carry):
-                to_cell = (g - (g // 2) * 2) * 8 + n
-
-                @pl.when(jnp.logical_or(to_img != img, to_cell != cell))
-                def _():
-                    send_message(msg, inbox, sems.at[4], sems.at[5], to_img, to_cell)
-
-                return carry
-
-            lax.fori_loop(0, 8, send_step, 0)
+            dy = pick(g, [STEPS[2 * n + side][0] for n in range(8)])
+            dz = pick(g, [STEPS[2 * n + side][1] for n in range(8)])
+
+            for q, (pi, pc, _) in enumerate(place.devices(dy, dz)):
+                copy = pltpu.make_async_remote_copy(
+                    src_ref=msg.at[pl.ds(pl.multiple_of(g * 128 + side * 64 + q * 8, 8), PAIRS)],
+                    dst_ref=inbox.at[pl.ds(pl.multiple_of(me * 8, 8), PAIRS)],
+                    send_sem=sems.at[4],
+                    recv_sem=sems.at[5],
+                    device_id=(pi, pc),
+                    device_id_type=MESH,
+                )
+                if side == 0 and q == 0:
+                    pl.when(g > 0)(copy.start)
+                else:
+                    copy.start()
         return carry
 
     lax.fori_loop(0, 8, reply_step, 0)
     own = pl.ds(pl.multiple_of(me * 8, 8), PAIRS)
-    inbox[own, :] = msg[own, :]
+    inbox[own, :] = msg[0:PAIRS, :]
 
     wait_rows(inbox, (DEVICES - 1) * PAIRS, sems.at[5])
 
@@ -863,29 +887,35 @@
         return carry
 
     lax.fori_loop(0, 4, back_pack, 0)
-    each_peer(
-        img,
-        cell,
-        lambda pi, pc: send_message(msg_back, inbox_back, sems.at[8], sems.at[9], pi, pc),
-    )
-    inbox_back[own, :] = msg_back[own, :]
+
+    def send_back(pi, pc, half, rank, group):
+        pltpu.make_async_remote_copy(
+            src_ref=msg_back.at[pl.ds(pl.multiple_of((pi * N_CELL + pc) * 8, 8), PAIRS)],
+            dst_ref=inbox_back.at[pl.ds(pl.multiple_of(rank * 8, 8), PAIRS)],
+            send_sem=sems.at[8],
+            recv_sem=back_sems.at[group],
+            device_id=(pi, pc),
+            device_id_type=MESH,
+        ).start()
+
+    each_step(place, send_back)
+    pltpu.make_async_copy(
+        msg_back.at[own], inbox_back.at[pl.ds(0, PAIRS)], back_sems.at[0]
+    ).start()
 
     acc[...] = jnp.zeros_like(acc)
-    wait_rows(inbox_back, (DEVICES - 1) * PAIRS, sems.at[9])
-
-    def owner_unpack(c, carry):
-        values = unpack_message(
-            inbox_back,
-            lambda i: pl.ds(c * 64 + i, 8, stride=8),
-            lambda i: pl.ds(512 + c * 64 + i, 8, stride=8),
-        )
-        for f in range(FEATS):
-            table[pl.ds(pl.multiple_of(f * ROWS + c * 8, 8), 8), :] = values[f]
-        return carry
-
-    lax.fori_loop(0, 8, owner_unpack, 0)
 
     def owner_step(k, carry):
+        for side in range(BLOCKS // 4):
+            g = k * (BLOCKS // 4) + side
+            wait_rows(inbox_back, 16 * PAIRS, back_sems.at[g])
+            values = unpack_message(
+                inbox_back,
+                lambda i: pl.ds(g * 128 + i, 8, stride=8),
+                lambda i: pl.ds(g * 128 + 64 + i, 8, stride=8),
+            )
+            for f in range(FEATS):
+                table[pl.ds(pl.multiple_of(f * ROWS + g * 8, 8), 8), :] = values[f]
         at = [k * 2 * BLOCKS + 2 * n for n in range(BLOCKS)]
         scatter_blocks(
             [row_pair(ids_own, a) for a in at],
@@ -995,9 +1025,11 @@
             pltpu.VMEM((2 * 3 * 48, 384), F32),
             pltpu.VMEM((2 * FEATS * 32, 256), F32),
             pltpu.SemaphoreType.DMA((11,)),
+            pltpu.SemaphoreType.DMA((8,)),
+            pltpu.SemaphoreType.DMA((8,)),
         ],
         compiler_params=pltpu.CompilerParams(
-            collective_id=0, has_side_effects=True, vmem_limit_bytes=56 * 1024 * 1024
+            collective_id=0, has_side_effects=True, vmem_limit_bytes=58 * 1024 * 1024
         ),
         name="splat_step",
     )(

time: 73 us -> 70.6 us (0.967)
  Pallas kernels: 72.8 us -> 70.4 us
    pallas_call x1, Pallas kernels: 68.2 us -> 65.8 us  [shards(): pl.pallas_call(step_kernel, out_shape=jax.ShapeDtypeStruct((FEATS * ROWS,...]
where the time goes in v4:
time: 70.6 us; the launch traced here: 70.4 us
  Pallas kernels  70.4 us (100%)
    pallas_call x1, Pallas kernels, shards(): pl.pallas_call(step_kernel, out_shape=jax.ShapeDtypeStruct((FEATS * ROWS,...  65.8 us
    pallas_call x1, Pallas kernels, shards(): pl.pallas_call(pullback_kernel, out_shape=jax.ShapeDtypeStruct(attributes...  4.55 us

profile of v4, /device:TPU:1, one launch (start us, length us, event | category | flops | bytes accessed | tf_op | source)
XLA Modules:
  0.0 70.4 jit_solution(5023878220141267041)
XLA Ops:
  0.0 65.8 %splat_step.1.feat_grad = f32[576,128]{1,0:T(8,128)} custom-call(f32[3,3]{1,0:T(4,128)} %cam_ref.3, s32[2,16]{1,0:T(2,128)} %len_ref.1, s32[64,128]{1,0:T(8,128)} %bitcast.2, f32[59,8192]{1,0:T(8,128)} %attr_hbm.3, f32[3,32,256]{2,1,0:T(8,128)} %target.1, s32[32,128]{1,0:T(8,128)} %bitcast.3), custom_call_target="tpu_custom_call" | custom-call | tf_op jit(solution)/shard_map/splat_step/pallas_call | solution.py:995
  65.8 4.6 %splat_pullback.1 = f32[59,8192]{1,0:T(8,128)} custom-call(f32[3,3]{1,0:T(4,128)} %cam_ref.3, f32[59,8192]{1,0:T(8,128)} %attr_hbm.3, f32[576,128]{1,0:T(8,128)} %splat_step.1.feat_grad), custom_call_target="tpu_custom_call" | custom-call | tf_op jit(solution)/shard_map/splat_pullback/pallas_call | solution.py:1043

commit v5 on v4

--- a/solution.py
+++ b/solution.py
@@ -523,25 +523,6 @@
     ).start()
     border_copies(ext_target, img, cell, sems.at[2], sems.at[3])
 
-    wait_rows(ext_target, BORDER_ROWS, sems.at[3])
-    for c in range(3):
-        for row_block in range(4):
-            for half in range(2):
-                strips = window(ext_target, img, cell, c, row_block, half)
-                for j in range(3):
-                    for m, v in ((3, strips[j]), (4, strips[j] * strips[j])):
-                        at = map_row(m, c) + 64 * j + 16 * row_block + 8 * half
-                        maps[at : at + 8, :] = v
-
-    def target_blur(c, carry):
-        for m in range(2):
-            for r in range(6):
-                at = pl.multiple_of((m * 3 + c) * 48 + 8 * r, 8)
-                blurred[pl.ds(at, 8), :] = blur(maps, map_row(3 + m, c) + 6 + 8 * r, 64)
-        return carry
-
-    lax.fori_loop(0, 3, target_blur, 0)
-
     odd = me - (me // 2) * 2
     left = left_half()
     left_row = lax.broadcasted_iota(I32, (1, 128), 1) < 64
@@ -595,6 +576,25 @@
     own = pl.ds(pl.multiple_of(me * 8, 8), PAIRS)
     inbox[own, :] = msg[0:PAIRS, :]
 
+    wait_rows(ext_target, BORDER_ROWS, sems.at[3])
+    for c in range(3):
+        for row_block in range(4):
+            for half in range(2):
+                strips = window(ext_target, img, cell, c, row_block, half)
+                for j in range(3):
+                    for m, v in ((3, strips[j]), (4, strips[j] * strips[j])):
+                        at = map_row(m, c) + 64 * j + 16 * row_block + 8 * half
+                        maps[at : at + 8, :] = v
+
+    def target_blur(c, carry):
+        for m in range(2):
+            for r in range(6):
+                at = pl.multiple_of((m * 3 + c) * 48 + 8 * r, 8)
+                blurred[pl.ds(at, 8), :] = blur(maps, map_row(3 + m, c) + 6 + 8 * r, 64)
+        return carry
+
+    lax.fori_loop(0, 3, target_blur, 0)
+
     wait_rows(inbox, (DEVICES - 1) * PAIRS, sems.at[5])
 
     def table_step(h, carry):
@@ -614,21 +614,21 @@
         got = gather_blocks(
             parts,
             thirds,
-            [row_pair(lists, k * 8 + 2 * n) for n in range(4)],
+            [row_pair(lists, k * 16 + 2 * n) for n in range(8)],
             [
-                hot_list[:, pl.ds(pl.multiple_of(k * 1024 + n * 256, 256), 256)]
-                for n in range(4)
+                hot_list[:, pl.ds(pl.multiple_of(k * 2048 + n * 256, 256), 256)]
+                for n in range(8)
             ],
         )
-        for n in range(4):
+        for n in range(8):
             for row in range(2):
                 for f in range(FEATS):
-                    entry[pl.ds(f * TILES + k * 8 + 2 * n + row, 1), :] = got[n][f][
+                    entry[pl.ds(f * TILES + k * 16 + 2 * n + row, 1), :] = got[n][f][
                         :, 128 * row : 128 * row + 128
                     ]
         return carry
 
-    lax.fori_loop(0, 4, list_step, 0)
+    lax.fori_loop(0, 2, list_step, 0)
 
     def entry_row(f, t):
         return entry[pl.ds(f * TILES + t, 1), :]
@@ -668,7 +668,7 @@
                         preferred_element_type=F32,
                     )
                 )
-                ratio[pixels_of(t), :] = alpha * jnp.exp(-logs)
+                ratio[pixels_of(t), :] = alpha
                 alphas.append(alpha)
             products = []
             for n, t in enumerate(tiles):
@@ -701,6 +701,13 @@
         ext_render[96 * k : 96 * k + 96, :] = picture[:, 128 * k : 128 * k + 128]
     pack_columns(ext_render)
     border_copies(ext_render, img, cell, sems.at[6], sems.at[7])
+
+    def ratio_step(t, carry):
+        alpha = ratio[pixels_of(t), :]
+        ratio[pixels_of(t), :] = alpha / (1.0 - alpha)
+        return carry
+
+    lax.fori_loop(0, TILES, ratio_step, 0)
     wait_rows(ext_render, BORDER_ROWS, sems.at[7])
 
     for c in range(3):

time: 70.6 us -> 67.5 us (0.956)
  Pallas kernels: 70.4 us -> 67.3 us
    pallas_call x1, Pallas kernels: 65.8 us -> 62.8 us  [shards(): pl.pallas_call(step_kernel, out_shape=jax.ShapeDtypeStruct((FEATS * ROWS,...]
where the time goes in v5:
time: 67.5 us; the launch traced here: 67.3 us
  Pallas kernels  67.3 us (100%)
    pallas_call x1, Pallas kernels, shards(): pl.pallas_call(step_kernel, out_shape=jax.ShapeDtypeStruct((FEATS * ROWS,...  62.8 us
    pallas_call x1, Pallas kernels, shards(): pl.pallas_call(pullback_kernel, out_shape=jax.ShapeDtypeStruct(attributes...  4.55 us

profile of v5, /device:TPU:1, one launch (start us, length us, event | category | flops | bytes accessed | tf_op | source)
XLA Modules:
  0.0 67.3 jit_solution(13479805420015420357)
XLA Ops:
  0.0 62.8 %splat_step.1.feat_grad = f32[576,128]{1,0:T(8,128)} custom-call(f32[3,3]{1,0:T(4,128)} %cam_ref.3, s32[2,16]{1,0:T(2,128)} %len_ref.1, s32[64,128]{1,0:T(8,128)} %bitcast.2, f32[59,8192]{1,0:T(8,128)} %attr_hbm.3, f32[3,32,256]{2,1,0:T(8,128)} %target.1, s32[32,128]{1,0:T(8,128)} %bitcast.3), custom_call_target="tpu_custom_call" | custom-call | tf_op jit(solution)/shard_map/splat_step/pallas_call | solution.py:1002
  62.8 4.6 %splat_pullback.1 = f32[59,8192]{1,0:T(8,128)} custom-call(f32[3,3]{1,0:T(4,128)} %cam_ref.3, f32[59,8192]{1,0:T(8,128)} %attr_hbm.3, f32[576,128]{1,0:T(8,128)} %splat_step.1.feat_grad), custom_call_target="tpu_custom_call" | custom-call | tf_op jit(solution)/shard_map/splat_pullback/pallas_call | solution.py:1050

commit v6 on v5

--- a/solution.py
+++ b/solution.py
@@ -413,13 +413,18 @@
 
 
 def step_kernel(
+    cam_hbm,
+    len_hbm,
+    vis_hbm,
+    attr_hbm,
+    target_hbm,
+    lists_hbm,
+    out,
     cam_ref,
     len_ref,
     vis,
-    attr_hbm,
     target,
     lists,
-    out,
     attr,
     arows,
     table,
@@ -449,6 +454,7 @@
     sems,
     id_sems,
     back_sems,
+    load_sems,
 ):
     img = lax.axis_index("img")
     cell = lax.axis_index("cell")
@@ -462,9 +468,23 @@
             barrier, 1, device_id=(pi, pc), device_id_type=MESH
         ),
     )
-    load_attr = pltpu.make_async_copy(attr_hbm, attr, sems.at[10])
-    load_attr.start()
-
+    load_target, load_lists, load_attr, load_cam, load_vis, load_len = loads = [
+        pltpu.make_async_copy(source, dest, load_sems.at[n])
+        for n, (source, dest) in enumerate(
+            (
+                (target_hbm, target),
+                (lists_hbm, lists),
+                (attr_hbm, attr),
+                (cam_hbm, cam_ref),
+                (vis_hbm, vis),
+                (len_hbm, len_ref),
+            )
+        )
+    ]
+    for load in loads:
+        load.start()
+
+    load_target.wait()
     for k in range(2):
         for t in range(2):
             for c in range(3):
@@ -474,6 +494,7 @@
                 ]
     pack_columns(ext_target)
 
+    load_lists.wait()
     def list_hot(b, carry):
         hot_list[:, pl.ds(pl.multiple_of(b * 256, 256), 256)] = one_hot(
             split_ids(row_pair(lists, b * 2))[1]
@@ -482,6 +503,7 @@
 
     lax.fori_loop(0, TILES // 2, list_hot, 0)
 
+    load_cam.wait()
     cam = read_camera(cam_ref)
     load_attr.wait()
     spread_rows(attr, arows)
@@ -505,6 +527,8 @@
         tri_before[128 * half : 128 * half + 128, :] = before
         tri_after[128 * half : 128 * half + 128, :] = after
 
+    load_vis.wait()
+    load_len.wait()
     pl.semaphore_wait(barrier, DEVICES - 1)
 
     def send_ids(pi, pc, half, rank, group):
@@ -952,9 +976,19 @@
     wait_rows(msg_back, (DEVICES - 1) * PAIRS, sems.at[8])
 
 
-def pullback_kernel(cam_ref, attr_hbm, feat_grad, out_hbm, attr, arows, result, load_sems, save_sem):
-    cam = read_camera(cam_ref)
-
+def pullback_kernel(
+    cam_hbm,
+    attr_hbm,
+    grad_hbm,
+    out_hbm,
+    cam_ref,
+    attr,
+    feat_grad,
+    arows,
+    result,
+    load_sems,
+    save_sem,
+):
     def block(h):
         return pl.ds(pl.multiple_of(h * 1024, 1024), 1024)
 
@@ -963,8 +997,16 @@
             attr_hbm.at[:, block(h)], attr.at[:, block(h)], load_sems.at[h]
         )
 
-    for h in range(8):
+    load_cam = pltpu.make_async_copy(cam_hbm, cam_ref, load_sems.at[8])
+    load_grad = pltpu.make_async_copy(grad_hbm, feat_grad, load_sems.at[9])
+    load(0).start()
+    load_cam.start()
+    load_grad.start()
+    for h in range(1, 8):
         load(h).start()
+    load_cam.wait()
+    load_grad.wait()
+    cam = read_camera(cam_ref)
 
     def step(h, carry):
         load(h).wait()
@@ -998,13 +1040,18 @@
 
 def shards(attributes, camera, target, visible_index, tile_lists, tile_len):
     vmem = pl.BlockSpec(memory_space=pltpu.VMEM)
-    smem = pl.BlockSpec(memory_space=pltpu.SMEM)
+    anywhere = pl.BlockSpec(memory_space=pl.ANY)
     feat_grad = pl.pallas_call(
         step_kernel,
         out_shape=jax.ShapeDtypeStruct((FEATS * ROWS, 128), F32),
-        in_specs=[smem, smem, vmem, pl.BlockSpec(memory_space=pl.ANY), vmem, vmem],
+        in_specs=[anywhere] * 6,
         out_specs=vmem,
         scratch_shapes=[
+            pltpu.SMEM((3, 3), F32),
+            pltpu.SMEM((2, 16), I32),
+            pltpu.VMEM((ROWS, 128), I32),
+            pltpu.VMEM((3, 32, 256), F32),
+            pltpu.VMEM((TILES, LIST), I32),
             pltpu.VMEM((ATTRS, 8192), F32),
             pltpu.VMEM((4096, 128), F32),
             pltpu.VMEM((FEATS * ROWS, 128), F32),
@@ -1031,9 +1078,10 @@
             pltpu.VMEM((3 * 3 * 3 * 48, 128), F32),
             pltpu.VMEM((2 * 3 * 48, 384), F32),
             pltpu.VMEM((2 * FEATS * 32, 256), F32),
-            pltpu.SemaphoreType.DMA((11,)),
+            pltpu.SemaphoreType.DMA((10,)),
             pltpu.SemaphoreType.DMA((8,)),
             pltpu.SemaphoreType.DMA((8,)),
+            pltpu.SemaphoreType.DMA((6,)),
         ],
         compiler_params=pltpu.CompilerParams(
             collective_id=0, has_side_effects=True, vmem_limit_bytes=58 * 1024 * 1024
@@ -1050,13 +1098,15 @@
     return pl.pallas_call(
         pullback_kernel,
         out_shape=jax.ShapeDtypeStruct(attributes.shape, F32),
-        in_specs=[smem, pl.BlockSpec(memory_space=pl.ANY), vmem],
-        out_specs=pl.BlockSpec(memory_space=pl.ANY),
+        in_specs=[anywhere] * 3,
+        out_specs=anywhere,
         scratch_shapes=[
+            pltpu.SMEM((3, 3), F32),
             pltpu.VMEM((ATTRS, 8192), F32),
+            pltpu.VMEM((FEATS * ROWS, 128), F32),
             pltpu.VMEM((512, 128), F32),
             pltpu.VMEM((ATTRS, 8192), F32),
-            pltpu.SemaphoreType.DMA((8,)),
+            pltpu.SemaphoreType.DMA((10,)),
             pltpu.SemaphoreType.DMA,
         ],
         name="splat_pullback",

time: 67.5 us -> 65.8 us (0.975)
  Pallas kernels: 67.3 us -> 65.6 us
    pallas_call x1, Pallas kernels: 4.55 us -> 3.69 us  [shards(): pl.pallas_call(pullback_kernel, out_shape=jax.ShapeDtypeStruct(attributes...]
    pallas_call x1, Pallas kernels: 62.8 us -> 61.9 us  [shards(): pl.pallas_call(step_kernel, out_shape=jax.ShapeDtypeStruct((FEATS * ROWS,...]
where the time goes in v6:
time: 65.8 us; the launch traced here: 65.6 us
  Pallas kernels  65.6 us (100%)
    pallas_call x1, Pallas kernels, shards(): pl.pallas_call(step_kernel, out_shape=jax.ShapeDtypeStruct((FEATS * ROWS,...  61.9 us
    pallas_call x1, Pallas kernels, shards(): pl.pallas_call(pullback_kernel, out_shape=jax.ShapeDtypeStruct(attributes...  3.69 us

profile of v6, /device:TPU:1, one launch (start us, length us, event | category | flops | bytes accessed | tf_op | source)
XLA Modules:
  0.0 65.6 jit_solution(16659772602749132700)
XLA Ops:
  0.0 61.9 %splat_step.1.grad_hbm = f32[576,128]{1,0:T(8,128)} custom-call(f32[3,3]{1,0:T(4,128)} %cam_hbm.3, s32[2,16]{1,0:T(2,128)} %len_hbm.1, s32[64,128]{1,0:T(8,128)} %bitcast.2, f32[59,8192]{1,0:T(8,128)} %attr_hbm.3, f32[3,32,256]{2,1,0:T(8,128)} %target_hbm.1, s32[32,128]{1,0:T(8,128)} %bitcast.3), custom_call_target="tpu_custom_call" | custom-call | tf_op jit(solution)/shard_map/splat_step/pallas_call | solution.py:1044
  61.9 3.7 %splat_pullback.1 = f32[59,8192]{1,0:T(8,128)} custom-call(f32[3,3]{1,0:T(4,128)} %cam_hbm.3, f32[59,8192]{1,0:T(8,128)} %attr_hbm.3, f32[576,128]{1,0:T(8,128)} %splat_step.1.grad_hbm), custom_call_target="tpu_custom_call" | custom-call | tf_op jit(solution)/shard_map/splat_pullback/pallas_call | solution.py:1098

commit v7 on v6

--- a/solution.py
+++ b/solution.py
@@ -24,7 +24,7 @@
 PAIRS = 5
 EXACT = 5
 BLOCKS = 8
-GROUP = 4
+GROUP = 8
 
 WEIGHT_SSIM = 0.2
 SMOOTHING = 0.01

time: 65.8 us -> 64.5 us (0.980)
  Pallas kernels: 65.6 us -> 64.3 us
    pallas_call x1, Pallas kernels: 61.9 us -> 60.6 us  [shards(): pl.pallas_call(step_kernel, out_shape=jax.ShapeDtypeStruct((FEATS * ROWS,...]
where the time goes in v7:
time: 64.5 us; the launch traced here: 64.3 us
  Pallas kernels  64.3 us (100%)
    pallas_call x1, Pallas kernels, shards(): pl.pallas_call(step_kernel, out_shape=jax.ShapeDtypeStruct((FEATS * ROWS,...  60.6 us
    pallas_call x1, Pallas kernels, shards(): pl.pallas_call(pullback_kernel, out_shape=jax.ShapeDtypeStruct(attributes...  3.69 us

profile of v7, /device:TPU:1, one launch (start us, length us, event | category | flops | bytes accessed | tf_op | source)
XLA Modules:
  0.0 64.3 jit_solution(5172611671404379328)
XLA Ops:
  0.0 60.6 %splat_step.1.grad_hbm = f32[576,128]{1,0:T(8,128)} custom-call(f32[3,3]{1,0:T(4,128)} %cam_hbm.3, s32[2,16]{1,0:T(2,128)} %len_hbm.1, s32[64,128]{1,0:T(8,128)} %bitcast.2, f32[59,8192]{1,0:T(8,128)} %attr_hbm.3, f32[3,32,256]{2,1,0:T(8,128)} %target_hbm.1, s32[32,128]{1,0:T(8,128)} %bitcast.3), custom_call_target="tpu_custom_call" | custom-call | tf_op jit(solution)/shard_map/splat_step/pallas_call | solution.py:1044
  60.6 3.7 %splat_pullback.1 = f32[59,8192]{1,0:T(8,128)} custom-call(f32[3,3]{1,0:T(4,128)} %cam_hbm.3, f32[59,8192]{1,0:T(8,128)} %attr_hbm.3, f32[576,128]{1,0:T(8,128)} %splat_step.1.grad_hbm), custom_call_target="tpu_custom_call" | custom-call | tf_op jit(solution)/shard_map/splat_pullback/pallas_call | solution.py:1098
